TPU v7x, 16 devices: a whole 2x2x2 slice. The times are simulated.
16 devices in a mesh: dp: 2 (over z), fsdp: 8 (over y, x, core).
Axes of the slice: x: 2, y: 2, z: 2, core: 2. Of those that a mesh axis runs over, the one named last changes fastest.
Arguments:
- hidden: bfloat16 [16, 1024, 960], P(('dp', 'fsdp'))
- cot_out: bfloat16 [16, 1024, 960], P(('dp', 'fsdp'))
- attn_norm: bfloat16 [2, 960], P(None, 'fsdp')
- w_query: bfloat16 [2, 960, 15, 64], P(None, 'fsdp')
- w_key: bfloat16 [2, 960, 5, 64], P(None, 'fsdp')
- w_value: bfloat16 [2, 960, 5, 64], P(None, 'fsdp')
- w_out: bfloat16 [2, 960, 960], P(None, 'fsdp')
- mlp_norm: bfloat16 [2, 960], P(None, 'fsdp')
- w_gate: bfloat16 [2, 960, 2560], P(None, 'fsdp')
- w_up: bfloat16 [2, 960, 2560], P(None, 'fsdp')
- w_down: bfloat16 [2, 2560, 960], P(None, 'fsdp')
Outputs:
- output 1: bfloat16 [16, 1024, 960], P(('dp', 'fsdp'))
- output 2: bfloat16 [16, 1024, 960], P(('dp', 'fsdp'))
- output 3: float32 [2, 960], P(None, 'fsdp')
- output 4: float32 [2, 960, 15, 64], P(None, 'fsdp')
- output 5: float32 [2, 960, 5, 64], P(None, 'fsdp')
- output 6: float32 [2, 960, 5, 64], P(None, 'fsdp')
- output 7: float32 [2, 960, 960], P(None, 'fsdp')
- output 8: float32 [2, 960], P(None, 'fsdp')
- output 9: float32 [2, 960, 2560], P(None, 'fsdp')
- output 10: float32 [2, 960, 2560], P(None, 'fsdp')
- output 11: float32 [2, 2560, 960], P(None, 'fsdp')
All inputs are finite; a program needn't handle non-finite values.
Results may differ from a plain program's by a relative error of at most 0.02.
Values are sent between devices in bfloat16 or wider.
A program may use at most 1 GiB of HBM per device.

v0:
```python
import functools
import math
import jax
import jax.numpy as jnp
from jax import lax
from jax.sharding import PartitionSpec as P, NamedSharding

NORM_EPS = 1e-5
ROPE_THETA = 500000.0
ROPE_FACTOR = 8.0
LOW_FACTOR = 1.0
HIGH_FACTOR = 4.0
OLD_CONTEXT = 8192.0
TOKEN_SPEC = P(('dp', 'fsdp'), None, None)
WEIGHT_SPECS = (P(None, 'fsdp'), P(None, 'fsdp', None, None), P(None, 'fsdp', None, None), P(None, 'fsdp', None, None), P(None, 'fsdp', None), P(None, 'fsdp'), P(None, 'fsdp', None), P(None, 'fsdp', None), P(None, 'fsdp', None))
MATRIX_IDS = (1, 2, 3, 4, 6, 7, 8)


def rope_tables(seq_len, head_dim):
    half_dim = head_dim // 2
    base_freq = 1.0 / (ROPE_THETA ** (jnp.arange(half_dim, dtype=jnp.float32) * 2.0 / head_dim))
    wave_len = 2.0 * math.pi / base_freq
    smooth = (OLD_CONTEXT / wave_len - LOW_FACTOR) / (HIGH_FACTOR - LOW_FACTOR)
    mid_freq = (1.0 - smooth) * base_freq / ROPE_FACTOR + smooth * base_freq
    scaled_freq = jnp.where(wave_len < OLD_CONTEXT / HIGH_FACTOR, base_freq, jnp.where(wave_len > OLD_CONTEXT / LOW_FACTOR, base_freq / ROPE_FACTOR, mid_freq))
    angles = jnp.arange(seq_len, dtype=jnp.float32)[:, None] * scaled_freq[None, :]
    return jnp.cos(angles), jnp.sin(angles)


def rms_norm(act_f32, norm_gain):
    inv_rms = lax.rsqrt(jnp.mean(act_f32 * act_f32, axis=-1, keepdims=True) + NORM_EPS)
    return (act_f32 * inv_rms * norm_gain).astype(jnp.bfloat16)


def apply_rope(act_f32, cos_t, sin_t):
    half_dim = act_f32.shape[-1] // 2
    low_half = act_f32[..., :half_dim]
    high_half = act_f32[..., half_dim:]
    cos_b = cos_t[:, None, :]
    sin_b = sin_t[:, None, :]
    return jnp.concatenate([low_half * cos_b - high_half * sin_b, high_half * cos_b + low_half * sin_b], axis=-1)


def attend(query_f, key_f, value_b, cos_t, sin_t):
    batch_size, seq_len, num_heads, head_dim = query_f.shape
    kv_heads = key_f.shape[2]
    query_rot = apply_rope(query_f, cos_t, sin_t).astype(jnp.bfloat16).reshape(batch_size, seq_len, kv_heads, num_heads // kv_heads, head_dim)
    key_rot = apply_rope(key_f, cos_t, sin_t).astype(jnp.bfloat16)
    scores = jnp.einsum('bskgd,btkd->bkgst', query_rot, key_rot, preferred_element_type=jnp.float32) * (head_dim ** -0.5)
    causal = jnp.arange(seq_len)[:, None] >= jnp.arange(seq_len)[None, :]
    scores = jnp.where(causal, scores, -1e30)
    attn_probs = jax.nn.softmax(scores, axis=-1).astype(jnp.bfloat16)
    attn_mix = jnp.einsum('bkgst,btkd->bskgd', attn_probs, value_b, preferred_element_type=jnp.float32)
    return attn_mix.astype(jnp.bfloat16).reshape(batch_size, seq_len, num_heads * head_dim)


def swiglu(gate_proj, up_proj):
    return (jax.nn.silu(gate_proj) * up_proj).astype(jnp.bfloat16)


def layer_forward(hidden, params, cos_t, sin_t):
    attn_gain, w_query, w_key, w_value, w_out, mlp_gain, w_gate, w_up, w_down = params
    hid_f32 = hidden.astype(jnp.float32)
    normed, norm_pull = jax.vjp(rms_norm, hid_f32, attn_gain.astype(jnp.float32))
    query_f = jnp.einsum('bsd,dhk->bshk', normed, w_query, preferred_element_type=jnp.float32)
    key_f = jnp.einsum('bsd,dhk->bshk', normed, w_key, preferred_element_type=jnp.float32)
    value_b = jnp.einsum('bsd,dhk->bshk', normed, w_value, preferred_element_type=jnp.float32).astype(jnp.bfloat16)
    attn_out, attn_pull = jax.vjp(functools.partial(attend, cos_t=cos_t, sin_t=sin_t), query_f, key_f, value_b)
    mid_hidden = (hid_f32 + jnp.einsum('bsf,fd->bsd', attn_out, w_out, preferred_element_type=jnp.float32)).astype(jnp.bfloat16)
    mid_f32 = mid_hidden.astype(jnp.float32)
    normed_mlp, norm_mlp_pull = jax.vjp(rms_norm, mid_f32, mlp_gain.astype(jnp.float32))
    gate_proj = jnp.einsum('bsd,df->bsf', normed_mlp, w_gate, preferred_element_type=jnp.float32)
    up_proj = jnp.einsum('bsd,df->bsf', normed_mlp, w_up, preferred_element_type=jnp.float32)
    mlp_act, mix_pull = jax.vjp(swiglu, gate_proj, up_proj)
    layer_out = (mid_f32 + jnp.einsum('bsf,fd->bsd', mlp_act, w_down, preferred_element_type=jnp.float32)).astype(jnp.bfloat16)
    saved_vals = (normed, norm_pull, attn_out, attn_pull, normed_mlp, norm_mlp_pull, mlp_act, mix_pull)
    return layer_out, saved_vals


def layer_backward(grad_out, saved_vals, matrices):
    w_query, w_key, w_value, w_out, w_gate, w_up, w_down = matrices
    normed, norm_pull, attn_out, attn_pull, normed_mlp, norm_mlp_pull, mlp_act, mix_pull = saved_vals
    grad_down = jnp.einsum('bsf,bsd->fd', mlp_act, grad_out, preferred_element_type=jnp.float32)
    grad_act = jnp.einsum('bsd,fd->bsf', grad_out, w_down, preferred_element_type=jnp.float32).astype(jnp.bfloat16)
    grad_gate_f, grad_up_f = mix_pull(grad_act)
    grad_gate_b = grad_gate_f.astype(jnp.bfloat16)
    grad_up_b = grad_up_f.astype(jnp.bfloat16)
    grad_gate = jnp.einsum('bsd,bsf->df', normed_mlp, grad_gate_b, preferred_element_type=jnp.float32)
    grad_up = jnp.einsum('bsd,bsf->df', normed_mlp, grad_up_b, preferred_element_type=jnp.float32)
    grad_normed_mlp = (jnp.einsum('bsf,df->bsd', grad_gate_b, w_gate, preferred_element_type=jnp.float32) + jnp.einsum('bsf,df->bsd', grad_up_b, w_up, preferred_element_type=jnp.float32)).astype(jnp.bfloat16)
    grad_mid_norm, grad_mlp_gain = norm_mlp_pull(grad_normed_mlp)
    grad_mid = (grad_out.astype(jnp.float32) + grad_mid_norm).astype(jnp.bfloat16)
    grad_wout = jnp.einsum('bsf,bsd->fd', attn_out, grad_mid, preferred_element_type=jnp.float32)
    grad_attn = jnp.einsum('bsd,fd->bsf', grad_mid, w_out, preferred_element_type=jnp.float32).astype(jnp.bfloat16)
    grad_query_f, grad_key_f, grad_value_b = attn_pull(grad_attn)
    grad_query_b = grad_query_f.astype(jnp.bfloat16)
    grad_key_b = grad_key_f.astype(jnp.bfloat16)
    grad_wq = jnp.einsum('bsd,bshk->dhk', normed, grad_query_b, preferred_element_type=jnp.float32)
    grad_wk = jnp.einsum('bsd,bshk->dhk', normed, grad_key_b, preferred_element_type=jnp.float32)
    grad_wv = jnp.einsum('bsd,bshk->dhk', normed, grad_value_b, preferred_element_type=jnp.float32)
    grad_normed = (jnp.einsum('bshk,dhk->bsd', grad_query_b, w_query, preferred_element_type=jnp.float32) + jnp.einsum('bshk,dhk->bsd', grad_key_b, w_key, preferred_element_type=jnp.float32) + jnp.einsum('bshk,dhk->bsd', grad_value_b, w_value, preferred_element_type=jnp.float32)).astype(jnp.bfloat16)
    grad_hid_norm, grad_attn_gain = norm_pull(grad_normed)
    grad_hidden = (grad_mid.astype(jnp.float32) + grad_hid_norm).astype(jnp.bfloat16)
    return grad_hidden, (grad_attn_gain, grad_wq, grad_wk, grad_wv, grad_wout, grad_mlp_gain, grad_gate, grad_up, grad_down)


def solution(mesh):
    device_count = mesh.shape['dp'] * mesh.shape['fsdp']

    def local_step(hidden, cot_out, attn_norm, w_query, w_key, w_value, w_out, mlp_norm, w_gate, w_up, w_down):
        shards = (attn_norm, w_query, w_key, w_value, w_out, mlp_norm, w_gate, w_up, w_down)
        num_layers = attn_norm.shape[0]
        cos_t, sin_t = rope_tables(hidden.shape[1], w_query.shape[-1])
        grad_scale = 1.0 / (hidden.shape[0] * hidden.shape[1] * device_count)
        hidden_act = hidden
        saved_all = []
        for layer_idx in range(num_layers):
            params = tuple(lax.all_gather(weight_shard[layer_idx], 'fsdp', axis=0, tiled=True) for weight_shard in shards)
            hidden_act, saved_vals = layer_forward(hidden_act, params, cos_t, sin_t)
            saved_all.append(saved_vals)
        grad_act = cot_out
        layer_grads = []
        for layer_idx in reversed(range(num_layers)):
            matrices = tuple(lax.all_gather(shards[param_idx][layer_idx], 'fsdp', axis=0, tiled=True) for param_idx in MATRIX_IDS)
            grad_act, local_grads = layer_backward(grad_act, saved_all[layer_idx], matrices)
            reduced = tuple(lax.psum(lax.psum_scatter(local_grad, 'fsdp', scatter_dimension=0, tiled=True), 'dp') * grad_scale for local_grad in local_grads)
            layer_grads.insert(0, reduced)
        stacked = tuple(jnp.stack([layer_grads[layer_idx][param_idx] for layer_idx in range(num_layers)]) for param_idx in range(len(shards)))
        return (hidden_act, grad_act) + stacked

    return jax.shard_map(local_step, mesh=mesh, in_specs=(TOKEN_SPEC, TOKEN_SPEC) + WEIGHT_SPECS, out_specs=(TOKEN_SPEC, TOKEN_SPEC) + WEIGHT_SPECS, check_vma=False)
```

profile of v0, /device:TPU:0, one launch (start us, length us, event | category | flops | bytes accessed | tf_op | source)
XLA Modules:
  0.0 1731.8 jit_solution(13149728757624323850)
XLA Ops:
  23.2 16.3 all-reduce.24
  46.1 18.6 %all-gather.2 = bf16[1,960,5,64]{3,2,0,1:T(8,128)(2,1)} all-gather(bf16[1,120,5,64]{3,2,0,1:T(8,128)(2,1)} %copy.71), channel_id=4, replica_groups=mesh['dp'=2,'fsdp'=8] {'fsdp'}, dimensions={1}, use_global_device_ids=true | all-gather | bytes 691200 | tf_op jit(solution)/shard_map/all_gather | solution.py:118
  67.6 18.6 %all-gather.1 = bf16[1,960,5,64]{3,2,0,1:T(8,128)(2,1)} all-gather(bf16[1,120,5,64]{3,2,0,1:T(8,128)(2,1)} %copy.70), channel_id=3, replica_groups=mesh['dp'=2,'fsdp'=8] {'fsdp'}, dimensions={1}, use_global_device_ids=true | all-gather | bytes 691200 | tf_op jit(solution)/shard_map/all_gather | solution.py:118
  94.4 21.1 %all-gather.10 = bf16[1,960,5,64]{3,2,0,1:T(8,128)(2,1)} all-gather(bf16[1,120,5,64]{3,2,0,1:T(8,128)(2,1)S(1)} %copy-done.49), channel_id=12, replica_groups=mesh['dp'=2,'fsdp'=8] {'fsdp'}, dimensions={1}, use_global_device_ids=true | all-gather | bytes 691200 | tf_op jit(solution)/shard_map/all_gather | solution.py:118
  118.4 20.7 %all-gather.11 = bf16[1,960,5,64]{3,2,0,1:T(8,128)(2,1)} all-gather(bf16[1,120,5,64]{3,2,0,1:T(8,128)(2,1)S(1)} %copy.74), channel_id=13, replica_groups=mesh['dp'=2,'fsdp'=8] {'fsdp'}, dimensions={1}, use_global_device_ids=true | all-gather | bytes 691200 | tf_op jit(solution)/shard_map/all_gather | solution.py:118
  155.9 25.8 %fusion.18 = (f32[5,3,1024]{2,1,0:T(4,128)S(1)}, f32[5,1024,1024,3]{2,1,3,0:T(8,128)}) fusion(pred[1024,1024]{0,1:T(8,128)(4,1)S(1)} %iota_compare_fusion, bf16[1024,5,3,32]{0,3,2,1:T(8,128)(2,1)} %bitcast.747, bf16[1024,5,3,32]{0,3,2,1:T(8,128)(2,1)} %bitcast.745, bf16[1024,5,32]{0,2,1:T(8,128)(2,1)} %get-tuple-element.69, ...), kind=kOutput, calls=%fused_computation.28 | convolution fusion | flops 2065679360 | bytes 66646016 | tf_op jit(solution)/shard_map/jvp(bskgd,btkd->bkgst)/dot_general | solution.py:49
  181.7 21.3 %fusion.118 = f32[5,3,1024]{2,1,0:T(4,128)S(1)} fusion(f32[5,3,1024]{2,1,0:T(4,128)S(1)} %get-tuple-element.92, f32[5,1024,1024,3]{2,1,3,0:T(8,128)} %get-tuple-element.93, pred[1024,1024]{0,1:T(8,128)(4,1)S(1)} %iota_compare_fusion), kind=kLoop, calls=%fused_computation.182 | loop fusion | flops 62899200 | bytes 64086016 | tf_op jit(solution)/shard_map/jvp()/reduce_sum | solution.py:52
  203.7 26.1 %fusion.166 = bf16[5,64,3,1024]{3,1,2,0:T(8,128)(2,1)} fusion(f32[1024,5,64]{0,2,1:T(8,128)} %bitcast.763, f32[5,3,1024]{2,1,0:T(4,128)S(1)} %fusion.118, f32[5,3,1024]{2,1,0:T(4,128)S(1)} %get-tuple-element.92, f32[5,1024,1024,3]{2,1,3,0:T(8,128)} %get-tuple-element.93, pred[1024,1024]{0,1:T(8,128)(4,1)S(1)} %iota_compare_fusion), kind=kOutput, calls=%fused_computation.226 | convolution fusion | flops 2093219840 | bytes 67362816 | tf_op jit(solution)/shard_map/jvp(bkgst,btkd->bskgd)/dot_general | solution.py:53
  241.6 10.8 fusion.66
  252.4 15.1 multiply_convert_fusion.1
  267.5 9.3 fusion.110
  285.4 25.7 %fusion.19 = (f32[5,3,1024]{2,1,0:T(4,128)S(1)}, f32[5,1024,1024,3]{2,1,3,0:T(8,128)}) fusion(pred[1024,1024]{0,1:T(8,128)(4,1)S(1)} %iota_compare_fusion, bf16[1024,5,3,32]{0,3,2,1:T(8,128)(2,1)} %bitcast.751, bf16[1024,5,3,32]{0,3,2,1:T(8,128)(2,1)} %bitcast.749, bf16[1024,5,32]{0,2,1:T(8,128)(2,1)} %get-tuple-element.67, ...), kind=kOutput, calls=%fused_computation.29 | convolution fusion | flops 2065679360 | bytes 66646016 | tf_op jit(solution)/shard_map/jvp(bskgd,btkd->bkgst)/dot_general | solution.py:49
  311.2 21.5 %fusion.119 = f32[5,3,1024]{2,1,0:T(4,128)S(1)} fusion(f32[5,3,1024]{2,1,0:T(4,128)S(1)} %get-tuple-element.100, f32[5,1024,1024,3]{2,1,3,0:T(8,128)} %get-tuple-element.101, pred[1024,1024]{0,1:T(8,128)(4,1)S(1)} %iota_compare_fusion), kind=kLoop, calls=%fused_computation.183 | loop fusion | flops 62899200 | bytes 64086016 | tf_op jit(solution)/shard_map/jvp()/reduce_sum | solution.py:52
  332.7 25.9 %fusion.169 = bf16[5,64,3,1024]{3,1,2,0:T(8,128)(2,1)} fusion(f32[1024,5,64]{0,2,1:T(8,128)} %bitcast.765, f32[5,3,1024]{2,1,0:T(4,128)S(1)} %fusion.119, f32[5,3,1024]{2,1,0:T(4,128)S(1)} %get-tuple-element.100, f32[5,1024,1024,3]{2,1,3,0:T(8,128)} %get-tuple-element.101, pred[1024,1024]{0,1:T(8,128)(4,1)S(1)} %iota_compare_fusion), kind=kOutput, calls=%fused_computation.227 | convolution fusion | flops 2093219840 | bytes 67362816 | tf_op jit(solution)/shard_map/jvp(bkgst,btkd->bskgd)/dot_general | solution.py:53
  365.3 11.4 fusion.54
  376.7 10.0 convolution_convert_fusion.3
  386.6 19.5 %fusion.40 = (bf16[1024,2560]{1,0:T(8,128)(2,1)S(1)}, bf16[1024,2560]{1,0:T(8,128)(2,1)}, bf16[1024,2560]{1,0:T(8,128)(2,1)}) fusion(f32[1024,2560]{1,0:T(8,128)} %fusion.54, bf16[1024,2560]{1,0:T(8,128)(2,1)} %convolution_convert_fusion.3, bf16[1,960,2560]{2,1,0:T(8,128)(2,1)} %all-gather.43.cloned.1.call-done, ...), kind=kOutput, calls=%fused_computation.54 | convolution fusion | flops 5081661440 | bytes 38346496 | tf_op jit(solution)/shard_map/bsd,df->bsf/dot_general | solution.py:72
  406.2 10.9 fusion.52
  417.1 6.4 fusion.85
  428.7 25.8 %fusion.188 = bf16[5,64,1024]{2,1,0:T(8,128)(2,1)} fusion(bf16[5,64,3,1024]{3,1,2,0:T(8,128)(2,1)S(1)} %bitcast.761, f32[5,3,1024]{2,1,0:T(4,128)S(1)} %fusion.119, f32[5,3,1024]{2,1,0:T(4,128)S(1)} %get-tuple-element.100, f32[5,1024,1024,3]{2,1,3,0:T(8,128)} %get-tuple-element.101, pred[1024,1024]{0,1:T(8,128)(4,1)S(1)} %iota_compare_fusion), kind=kOutput, calls=%fused_computation.232 | convolution fusion | flops 2092236800 | bytes 66707456 | tf_op jit(solution)/shard_map/transpose(jvp(bkgst,btkd->bskgd))/dot_general | solution.py:53
  454.5 37.2 %fusion.8 = (f32[5,3,1024]{2,1,0:T(4,128)S(1)}, bf16[5,3,1024,1024]{2,3,1,0:T(8,128)(2,1)}) fusion(f32[5,3,1024]{2,1,0:T(4,128)S(1)} %copy-done.62, f32[5,3,1024]{2,1,0:T(4,128)S(1)} %get-tuple-element.100, f32[5,1024,1024,3]{2,1,3,0:T(8,128)} %get-tuple-element.101, pred[1024,1024]{0,1:T(8,128)(4,1)S(1)} %iota_compare_fusion, ...), kind=kOutput, calls=%fused_computation.12 | convolution fusion | flops 2139407360 | bytes 98881536 | tf_op jit(solution)/shard_map/transpose(jvp(bkgst,btkd->bskgd))/dot_general | solution.py:53
  491.8 36.8 %convert_bitcast_fusion.5 = f32[1,1024,5,64]{1,3,2,0:T(8,128)} fusion(bf16[5,3,1024,1024]{2,3,1,0:T(8,128)(2,1)} %get-tuple-element.106, f32[5,3,1024]{2,1,0:T(4,128)S(1)} %neg.37, f32[5,3,1024]{2,1,0:T(4,128)S(1)} %fusion.119, pred[1024,1024]{0,1:T(8,128)(4,1)S(1)} %iota_compare_fusion, f32[5,3,1024]{2,1,0:T(4,128)S(1)} %get-tuple-element.100, ...), kind=kOutput, calls=%fused_computation.237 | convolution fusion | flops 2159411200 | bytes 98881536 | tf_op jit(solution)/shard_map/transpose(jvp(bskgd,btkd->bkgst))/dot_general | solution.py:49
  528.6 35.5 %bitcast_convert_fusion.1 = f32[1,5,1024,3,64]{2,4,3,1,0:T(8,128)S(1)} fusion(bf16[5,3,1024,1024]{2,3,1,0:T(8,128)(2,1)} %get-tuple-element.106, f32[5,3,1024]{2,1,0:T(4,128)S(1)} %neg.37, f32[5,3,1024]{2,1,0:T(4,128)S(1)} %fusion.119, pred[1024,1024]{0,1:T(8,128)(4,1)S(1)} %iota_compare_fusion, f32[5,3,1024]{2,1,0:T(4,128)S(1)} %get-tuple-element.100, ...), kind=kOutput, calls=%fused_computation.202 | convolution fusion | flops 2158100480 | bytes 100192256 | tf_op jit(solution)/shard_map/transpose(jvp(bskgd,btkd->bkgst))/dot_general | solution.py:49
  581.3 17.9 %fusion.43 = (bf16[1024,2560]{1,0:T(8,128)(2,1)}, bf16[1024,2560]{1,0:T(8,128)(2,1)}) fusion(f32[1024,2560]{1,0:T(8,128)} %fusion.66, f32[1024,2560]{1,0:T(8,128)} %get-tuple-element.97, bf16[1,2560,960]{2,1,0:T(8,128)(2,1)} %all-gather.37.cloned.1.call-done, bf16[1,1024,960]{1,2,0:T(8,128)(2,1)S(1)} %fusion.99), kind=kOutput, calls=%fused_computation.57 | convolution fusion | flops 5075107840 | bytes 38338560 | tf_op jit(solution)/shard_map/bsd,fd->bsf/dot_general | solution.py:84
  599.3 9.2 fusion.60
  608.5 8.8 fusion.89
  622.4 25.4 %fusion.191 = bf16[5,64,1024]{2,1,0:T(8,128)(2,1)} fusion(bf16[5,64,3,1024]{3,1,2,0:T(8,128)(2,1)} %bitcast.759, f32[5,3,1024]{2,1,0:T(4,128)S(1)} %copy-done.54, f32[5,3,1024]{2,1,0:T(4,128)S(1)} %copy-done.60, f32[5,1024,1024,3]{2,1,3,0:T(8,128)} %get-tuple-element.93, pred[1024,1024]{0,1:T(8,128)(4,1)S(1)} %iota_compare_fusion), kind=kOutput, calls=%fused_computation.233 | convolution fusion | flops 2092236800 | bytes 66707456 | tf_op jit(solution)/shard_map/transpose(jvp(bkgst,btkd->bskgd))/dot_general | solution.py:53
  651.0 37.4 %fusion.17 = (f32[5,3,1024]{2,1,0:T(4,128)S(1)}, bf16[5,3,1024,1024]{2,3,1,0:T(8,128)(2,1)}) fusion(f32[5,3,1024]{2,1,0:T(4,128)S(1)} %copy-done.61, f32[5,3,1024]{2,1,0:T(4,128)S(1)} %copy-done.60, f32[5,1024,1024,3]{2,1,3,0:T(8,128)} %get-tuple-element.93, pred[1024,1024]{0,1:T(8,128)(4,1)S(1)} %iota_compare_fusion, ...), kind=kOutput, calls=%fused_computation.21 | convolution fusion | flops 2139407360 | bytes 98881536 | tf_op jit(solution)/shard_map/transpose(jvp(bkgst,btkd->bskgd))/dot_general | solution.py:53
  688.5 36.0 %convert_bitcast_fusion.4 = f32[1,1024,5,64]{1,3,2,0:T(8,128)S(1)} fusion(bf16[5,3,1024,1024]{2,3,1,0:T(8,128)(2,1)} %get-tuple-element.110, f32[5,3,1024]{2,1,0:T(4,128)S(1)} %neg.40, f32[5,3,1024]{2,1,0:T(4,128)S(1)} %copy-done.54, pred[1024,1024]{0,1:T(8,128)(4,1)S(1)} %iota_compare_fusion, f32[5,3,1024]{2,1,0:T(4,128)S(1)} %copy-done.60, ...), kind=kOutput, calls=%fused_computation.236 | convolution fusion | flops 2159411200 | bytes 98881536 | tf_op jit(solution)/shard_map/transpose(jvp(bskgd,btkd->bkgst))/dot_general | solution.py:49
  734.1 36.4 %bitcast_convert_fusion = f32[1,5,1024,3,64]{2,4,3,1,0:T(8,128)S(1)} fusion(bf16[5,3,1024,1024]{2,3,1,0:T(8,128)(2,1)} %get-tuple-element.110, f32[5,3,1024]{2,1,0:T(4,128)S(1)} %neg.40, f32[5,3,1024]{2,1,0:T(4,128)S(1)} %copy-done.54, pred[1024,1024]{0,1:T(8,128)(4,1)S(1)} %iota_compare_fusion, f32[5,3,1024]{2,1,0:T(4,128)S(1)} %copy-done.60, ...), kind=kOutput, calls=%fused_computation.192 | convolution fusion | flops 2158100480 | bytes 100192256 | tf_op jit(solution)/shard_map/transpose(jvp(bskgd,btkd->bkgst))/dot_general | solution.py:49
  790.4 10.9 fusion.258
  801.4 11.2 fusion.260
  812.7 10.6 fusion.143
  823.3 11.0 fusion.134
  835.0 10.6 fusion.264
  845.7 10.7 fusion.266
  863.3 44.4 %reduce-scatter.35.cloned.1.call-done = f32[120,960]{1,0:T(8,128)} async-done(((f32[960,960]{1,0:T(8,128)}), f32[120,960]{1,0:T(8,128)}) %reduce-scatter.35.cloned.1.call-update) | async-done | bytes 460816
  909.8 45.5 %reduce-scatter.21.cloned.1.call-done = f32[120,960]{1,0:T(8,128)} async-done(((f32[960,960]{1,0:T(8,128)}), f32[120,960]{1,0:T(8,128)}) %reduce-scatter.21.cloned.1.call-update) | async-done | bytes 460816 | tf_op jit(solution)/shard_map/reduce_scatter | solution.py:126
  955.3 47.6 %reduce-scatter.19.cloned.1.call-done = f32[120,960]{1,0:T(8,128)} async-done(((f32[960,960]{1,0:T(8,128)}), f32[120,960]{1,0:T(8,128)}) %reduce-scatter.19.cloned.1.call-update) | async-done | bytes 460816 | tf_op jit(solution)/shard_map/reduce_scatter | solution.py:126
  1002.9 76.5 %reduce-scatter.29.cloned.1.call-done = f32[120,2560]{1,0:T(8,128)} async-done(((f32[960,2560]{1,0:T(8,128)}), f32[120,2560]{1,0:T(8,128)}) %reduce-scatter.29.cloned.1.call-update) | async-done | bytes 1228816 | tf_op jit(solution)/shard_map/reduce_scatter | solution.py:126
  1079.4 76.5 %reduce-scatter.25.cloned.1.call-done = f32[120,2560]{1,0:T(8,128)} async-done(((f32[960,2560]{1,0:T(8,128)}), f32[120,2560]{1,0:T(8,128)}) %reduce-scatter.25.cloned.1.call-update) | async-done | bytes 1228816 | tf_op jit(solution)/shard_map/reduce_scatter | solution.py:126
  1155.8 79.7 %reduce-scatter.33.cloned.1.call-done = f32[320,960]{1,0:T(8,128)} async-done(((f32[2560,960]{1,0:T(8,128)}), f32[320,960]{1,0:T(8,128)}) %reduce-scatter.33.cloned.1.call-update) | async-done | bytes 1228816 | tf_op jit(solution)/shard_map/reduce_scatter | solution.py:126
  1235.5 79.8 %reduce-scatter.31.cloned.1.call-done = f32[320,960]{1,0:T(8,128)} async-done(((f32[2560,960]{1,0:T(8,128)}), f32[320,960]{1,0:T(8,128)}) %reduce-scatter.31.cloned.1.call-update) | async-done | bytes 1228816 | tf_op jit(solution)/shard_map/reduce_scatter | solution.py:126
  1315.3 76.5 %reduce-scatter.27.cloned.1.call-done = f32[120,2560]{1,0:T(8,128)} async-done(((f32[960,2560]{1,0:T(8,128)}), f32[120,2560]{1,0:T(8,128)}) %reduce-scatter.27.cloned.1.call-update) | async-done | bytes 1228816 | tf_op jit(solution)/shard_map/reduce_scatter | solution.py:126
  1391.8 76.6 %reduce-scatter.23.cloned.1.call-done = f32[120,2560]{1,0:T(8,128)} async-done(((f32[960,2560]{1,0:T(8,128)}), f32[120,2560]{1,0:T(8,128)}) %reduce-scatter.23.cloned.1.call-update) | async-done | bytes 1228816 | tf_op jit(solution)/shard_map/reduce_scatter | solution.py:126
  1477.8 23.1 %all-reduce.20 = (f32[960]{0:T(1024)S(1)}, f32[960]{0:T(1024)S(1)}, f32[960]{0:T(1024)S(1)}, f32[960]{0:T(1024)S(1)}) all-reduce(f32[960]{0:T(1024)S(1)} %copy-done.75, f32[960]{0:T(1024)S(1)} %get-tuple-element.15, f32[960]{0:T(1024)S(1)} %copy-done.90, f32[960]{0:T(1024)S(1)} %copy-done.91), channel_id=21, replica_groups=mesh['dp'=2,'fsdp'=8] {'fsdp'}, use_global_device_ids=true, to_apply=%region_18.19.clone | all-reduce | flops 3840 | bytes 30720
  1512.9 9.7 fusion.114
  1522.6 184.1 %all-reduce.30.cloned.1.call-done = (f32[120,15,64]{0,2,1:T(8,128)}, f32[120,15,64]{0,2,1:T(8,128)}, f32[120,5,64]{0,2,1:T(8,128)}, f32[120,5,64]{0,2,1:T(8,128)...) async-done(((f32[120,15,64]{0,2,1:T(8,128)}, ...) | async-done | bytes 9830416 | tf_op jit(solution)/shard_map/psum | solution.py:126
  (382 shorter events, 187.8 us)
Async XLA Ops:
  7.2 137.1 %all-gather.29.cloned.1.call-start = ((), (), s32[]{:S(2)}) async-start(), calls=%async_computation.18 | async-start | bytes 4423680 | tf_op jit(solution)/shard_map/all_gather | solution.py:118
  9.6 220.2 %all-gather.31.cloned.1.call-start = ((), (), s32[]{:S(2)}) async-start(), calls=%async_computation.19 | async-start | bytes 2211840 | tf_op jit(solution)/shard_map/all_gather | solution.py:118
  11.6 224.3 %all-gather.39.cloned.1.call-start = ((), (), s32[]{:S(2)}) async-start(), calls=%async_computation.23 | async-start | bytes 4423680 | tf_op jit(solution)/shard_map/all_gather | solution.py:118
  12.8 228.9 %all-gather.33.cloned.1.call-start = ((), (), s32[]{:S(2)}) async-start(), calls=%async_computation.20 | async-start | bytes 5529600 | tf_op jit(solution)/shard_map/all_gather | solution.py:118
  14.0 238.4 %all-gather.35.cloned.1.call-start = ((), (), s32[]{:S(2)}) async-start(), calls=%async_computation.21 | async-start | bytes 5529600 | tf_op jit(solution)/shard_map/all_gather | solution.py:118
  16.5 24.7 %copy-start.58 = (bf16[2,120,5,64]{1,3,2,0:T(8,128)(2,1)S(1)}, bf16[2,120,5,64]{1,3,2,0:T(8,128)(2,1)}, u32[]{:S(2)}) copy-start(bf16[2,120,5,64]{1,3,2,0:T(8,128)(2,1)} %param.15) | copy-start | bytes 460804
  16.6 251.0 %all-gather.37.cloned.1.call-start = ((), (), s32[]{:S(2)}) async-start(), calls=%async_computation.22 | async-start | bytes 5898240 | tf_op jit(solution)/shard_map/all_gather | solution.py:118
  17.8 340.8 %all-gather.41.cloned.1.call-start = ((), (), s32[]{:S(2)}) async-start(), calls=%async_computation.24 | async-start | bytes 2211840 | tf_op jit(solution)/shard_map/all_gather | solution.py:118
  18.5 346.8 %all-gather.45.cloned.1.call-start = ((), (), s32[]{:S(2)}) async-start(), calls=%async_computation.26 | async-start | bytes 5529600 | tf_op jit(solution)/shard_map/all_gather | solution.py:118
  19.3 357.4 %all-gather.47.cloned.1.call-start = ((), (), s32[]{:S(2)}) async-start(), calls=%async_computation.27 | async-start | bytes 5898240 | tf_op jit(solution)/shard_map/all_gather | solution.py:118
  20.0 366.6 %all-gather.43.cloned.1.call-start = ((), (), s32[]{:S(2)}) async-start(), calls=%async_computation.25 | async-start | bytes 5529600 | tf_op jit(solution)/shard_map/all_gather | solution.py:118
  20.6 836.8 %all-reduce.28.cloned.1.call-start = ((), (), s32[]{:S(2)}) async-start(), calls=%async_computation.30 | async-start | bytes 10485760
  39.5 110.5 %copy-start.63 = (f32[960]{0:T(1024)}, f32[960]{0:T(1024)S(1)}, u32[]{:S(2)}) copy-start(f32[960]{0:T(1024)S(1)} %convert_element_type.444) | copy-start | bytes 11524
  40.1 212.3 %copy-start.76 = (f32[960]{0:T(1024)}, f32[960]{0:T(1024)S(1)}, u32[]{:S(2)}) copy-start(f32[960]{0:T(1024)S(1)} %convert_element_type.445) | copy-start | bytes 11524
  41.2 108.8 %copy-start.65 = (f32[1024]{0:T(1024)}, f32[1024]{0:T(1024)S(1)}, u32[]{:S(2)}) copy-start(f32[1024]{0:T(1024)S(1)} %fusion.236) | copy-start | bytes 12292
  46.1 107.8 %copy-start.2 = (f32[1024,32]{0,1:T(8,128)}, f32[1024,32]{0,1:T(8,128)S(1)}, u32[]{:S(2)}) copy-start(f32[1024,32]{0,1:T(8,128)S(1)} %get-tuple-element.86) | copy-start | bytes 393220
  46.1 107.8 %copy-start.6 = (f32[1024,32]{0,1:T(8,128)}, f32[1024,32]{0,1:T(8,128)S(1)}, u32[]{:S(2)}) copy-start(f32[1024,32]{0,1:T(8,128)S(1)} %get-tuple-element.87) | copy-start | bytes 393220
  203.0 26.8 %copy-start.53 = (f32[5,3,1024]{2,1,0:T(4,128)}, f32[5,3,1024]{2,1,0:T(4,128)S(1)}, u32[]{:S(2)}) copy-start(f32[5,3,1024]{2,1,0:T(4,128)S(1)} %fusion.118) | copy-start | bytes 184324
  276.9 81.8 %copy-start.10 = (bf16[1,1024,960]{1,2,0:T(8,128)(2,1)}, bf16[1,1024,960]{1,2,0:T(8,128)(2,1)S(1)}, u32[]{:S(2)}) copy-start(bf16[1,1024,960]{1,2,0:T(8,128)(2,1)S(1)} %get-tuple-element.99) | copy-start | bytes 5898244
  364.6 58.9 %copy-start.84 = (f32[1024]{0:T(1024)}, f32[1024]{0:T(1024)S(1)}, u32[]{:S(2)}) copy-start(f32[1024]{0:T(1024)S(1)} %fusion.239) | copy-start | bytes 12292
  428.7 25.8 %copy-start.62 = (f32[5,3,1024]{2,1,0:T(4,128)S(1)}, f32[5,3,1024]{2,1,0:T(4,128)}, u32[]{:S(2)}) copy-start(f32[5,3,1024]{2,1,0:T(4,128)} %multiply_divide_fusion.1) | copy-start | bytes 184324
  454.5 37.2 %copy-start.47 = (bf16[1,1024,15,32]{1,3,2,0:T(8,128)(2,1)S(1)}, bf16[1,1024,15,32]{1,3,2,0:T(8,128)(2,1)}, u32[]{:S(2)}) copy-start(bf16[1,1024,15,32]{1,3,2,0:T(8,128)(2,1)} %get-tuple-element.58) | copy-start | bytes 2949124
  454.5 37.2 %copy-start.48 = (bf16[1,1024,15,32]{1,3,2,0:T(8,128)(2,1)S(1)}, bf16[1,1024,15,32]{1,3,2,0:T(8,128)(2,1)}, u32[]{:S(2)}) copy-start(bf16[1,1024,15,32]{1,3,2,0:T(8,128)(2,1)} %get-tuple-element.59) | copy-start | bytes 2949124
  491.8 36.8 %copy-start.56 = (bf16[1024,5,32]{0,2,1:T(8,128)(2,1)S(1)}, bf16[1024,5,32]{0,2,1:T(8,128)(2,1)}, u32[]{:S(2)}) copy-start(bf16[1024,5,32]{0,2,1:T(8,128)(2,1)} %copy-done.55) | copy-start | bytes 983044
  491.8 36.8 %copy-start.57 = (bf16[1024,5,32]{0,2,1:T(8,128)(2,1)S(1)}, bf16[1024,5,32]{0,2,1:T(8,128)(2,1)}, u32[]{:S(2)}) copy-start(bf16[1024,5,32]{0,2,1:T(8,128)(2,1)} %get-tuple-element.67) | copy-start | bytes 983044
  528.6 35.6 %copy-start.11 = (bf16[1,1024,960]{1,2,0:T(8,128)(2,1)S(1)}, bf16[1,1024,960]{1,2,0:T(8,128)(2,1)}, u32[]{:S(2)}) copy-start(bf16[1,1024,960]{1,2,0:T(8,128)(2,1)} %copy-done.10) | copy-start | bytes 5898244
  528.6 35.6 %copy-start.68 = (f32[960]{0:T(1024)S(1)}, f32[960]{0:T(1024)}, u32[]{:S(2)}) copy-start(f32[960]{0:T(1024)} %convert_element_type.446) | copy-start | bytes 11524
  528.6 35.6 %copy-start.71 = (f32[1024]{0:T(1024)S(1)}, f32[1024]{0:T(1024)}, u32[]{:S(2)}) copy-start(f32[1024]{0:T(1024)} %copy-done.70) | copy-start | bytes 12292
  581.3 36.0 %copy-start.13 = (bf16[1,1024,960]{1,2,0:T(8,128)(2,1)}, bf16[1,1024,960]{1,2,0:T(8,128)(2,1)S(1)}, u32[]{:S(2)}) copy-start(bf16[1,1024,960]{1,2,0:T(8,128)(2,1)S(1)} %fusion.99) | copy-start | bytes 5898244
  622.4 25.5 %copy-start.1 = (bf16[1,1024,960]{1,2,0:T(8,128)(2,1)S(1)}, bf16[1,1024,960]{1,2,0:T(8,128)(2,1)}, u32[]{:S(2)}) copy-start(bf16[1,1024,960]{1,2,0:T(8,128)(2,1)} %param.11) | copy-start | bytes 5898244
  622.4 25.5 %copy-start.64 = (f32[960]{0:T(1024)S(1)}, f32[960]{0:T(1024)}, u32[]{:S(2)}) copy-start(f32[960]{0:T(1024)} %copy-done.63) | copy-start | bytes 11524
  622.4 25.5 %copy-start.66 = (f32[1024]{0:T(1024)S(1)}, f32[1024]{0:T(1024)}, u32[]{:S(2)}) copy-start(f32[1024]{0:T(1024)} %copy-done.65) | copy-start | bytes 12292
  651.0 37.4 %copy-start.45 = (bf16[1,1024,15,32]{1,3,2,0:T(8,128)(2,1)S(1)}, bf16[1,1024,15,32]{1,3,2,0:T(8,128)(2,1)}, u32[]{:S(2)}) copy-start(bf16[1,1024,15,32]{1,3,2,0:T(8,128)(2,1)} %get-tuple-element.60) | copy-start | bytes 2949124
  651.0 37.4 %copy-start.46 = (bf16[1,1024,15,32]{1,3,2,0:T(8,128)(2,1)S(1)}, bf16[1,1024,15,32]{1,3,2,0:T(8,128)(2,1)}, u32[]{:S(2)}) copy-start(bf16[1,1024,15,32]{1,3,2,0:T(8,128)(2,1)} %get-tuple-element.61) | copy-start | bytes 2949124
  688.5 36.1 %copy-start.5 = (f32[1024,32]{0,1:T(8,128)S(1)}, f32[1024,32]{0,1:T(8,128)}, u32[]{:S(2)}) copy-start(f32[1024,32]{0,1:T(8,128)} %copy-done.2) | copy-start | bytes 393220
  688.5 36.1 %copy-start.9 = (f32[1024,32]{0,1:T(8,128)S(1)}, f32[1024,32]{0,1:T(8,128)}, u32[]{:S(2)}) copy-start(f32[1024,32]{0,1:T(8,128)} %copy-done.6) | copy-start | bytes 393220
  727.0 134.4 %reduce-scatter.37.cloned.1.call-start = ((), (), s32[]{:S(2)}) async-start(), calls=%async_computation.29 | async-start | bytes 4423680
  734.0 173.7 %reduce-scatter.35.cloned.1.call-start = ((), (), s32[]{:S(2)}) async-start(), calls=%async_computation.28 | async-start | bytes 4423680
  776.9 178.4 %reduce-scatter.21.cloned.1.call-start = ((), (), s32[]{:S(2)}) async-start(), calls=%async_computation.11 | async-start | bytes 4423680 | tf_op jit(solution)/shard_map/reduce_scatter | solution.py:126
  783.3 219.6 %reduce-scatter.19.cloned.1.call-start = ((), (), s32[]{:S(2)}) async-start(), calls=%async_computation.10 | async-start | bytes 4423680 | tf_op jit(solution)/shard_map/reduce_scatter | solution.py:126
  789.7 289.7 %reduce-scatter.29.cloned.1.call-start = ((), (), s32[]{:S(2)}) async-start(), calls=%async_computation.15 | async-start | bytes 11059200 | tf_op jit(solution)/shard_map/reduce_scatter | solution.py:126
  801.3 354.5 %reduce-scatter.25.cloned.1.call-start = ((), (), s32[]{:S(2)}) async-start(), calls=%async_computation.13 | async-start | bytes 11059200 | tf_op jit(solution)/shard_map/reduce_scatter | solution.py:126
  812.6 422.9 %reduce-scatter.33.cloned.1.call-start = ((), (), s32[]{:S(2)}) async-start(), calls=%async_computation.17 | async-start | bytes 11796480 | tf_op jit(solution)/shard_map/reduce_scatter | solution.py:126
  823.3 492.1 %reduce-scatter.31.cloned.1.call-start = ((), (), s32[]{:S(2)}) async-start(), calls=%async_computation.16 | async-start | bytes 11796480 | tf_op jit(solution)/shard_map/reduce_scatter | solution.py:126
  834.4 557.4 %reduce-scatter.27.cloned.1.call-start = ((), (), s32[]{:S(2)}) async-start(), calls=%async_computation.14 | async-start | bytes 11059200 | tf_op jit(solution)/shard_map/reduce_scatter | solution.py:126
  845.7 622.7 %reduce-scatter.23.cloned.1.call-start = ((), (), s32[]{:S(2)}) async-start(), calls=%async_computation.12 | async-start | bytes 11059200 | tf_op jit(solution)/shard_map/reduce_scatter | solution.py:126
  856.5 850.3 %all-reduce.30.cloned.1.call-start = ((), (), s32[]{:S(2)}) async-start(), calls=%async_computation.31 | async-start | bytes 20316160 | tf_op jit(solution)/shard_map/psum | solution.py:126
  1474.2 33.5 %copy-start.74 = (f32[1024]{0:T(1024)S(1)}, f32[1024]{0:T(1024)}, u32[]{:S(2)}) copy-start(f32[1024]{0:T(1024)} %copy-done.73) | copy-start | bytes 12292
  (75 other events, 357.4 us)
Sparse Core Ops, SparseCore 0:
  10.4 34.7 all-gather.28
  47.6 25.7 all-gather.30
  75.8 36.8 all-gather.38
  114.4 39.8 all-gather.32
  156.0 35.8 all-gather.34
  194.1 37.2 all-gather.36
  233.2 23.4 all-gather.40
  258.6 35.8 all-gather.44
  296.3 37.2 all-gather.46
  335.3 35.8 all-gather.42
  727.1 85.2 all-reduce.27
  815.7 44.2 reduce-scatter.36
  863.5 44.2 reduce-scatter.34
  911.1 44.1 reduce-scatter.20
  958.6 44.2 reduce-scatter.18
  1006.3 73.0 reduce-scatter.28
  1082.7 73.0 reduce-scatter.24
  1159.1 76.3 reduce-scatter.32
  1239.0 76.3 reduce-scatter.30
  1318.7 73.0 reduce-scatter.26
  1395.3 73.0 reduce-scatter.22
  1474.0 232.7 all-reduce.29
where the time goes:
time: 1740 us; the launch traced here: 1730 us
  waiting for transfers between devices  790 us (45%)
  matrix products  658 us (38%)
  blocking collectives  124 us (7%)
  other arithmetic  82.7 us (5%)
  local copies, waits for them, and re-layouts  59.2 us (3%)
    reduce_scatter x8, waiting for transfers between devices, local_step(): lax.psum_scatter(local_grad, 'fsdp', scatter_dimension=0, tiled=True)  559 us
    dot_general x6, matrix products, attend(): jnp.einsum('bskgd,btkd->bkgst', query_rot, key_rot, preferred_element_typ...  196 us
    psum x1, waiting for transfers between devices, local_step(): lax.psum(lax.psum_scatter(local_grad, 'fsdp', scatter_dimension=0, tiled=...  184 us
    dot_general x6, matrix products, attend(): jnp.einsum('bkgst,btkd->bskgd', attn_probs, value_b, preferred_element_ty...  178 us
    all_gather x4, blocking collectives, local_step(): lax.all_gather(weight_shard[layer_idx], 'fsdp', axis=0, tiled=True)  79 us
    unnamed x25, waiting for transfers between devices  47.3 us
    reduce_sum x2, other arithmetic, attend(): attn_probs = jax.nn.softmax(scores, axis=-1).astype(jnp.bfloat16)  42.8 us
    unnamed x2, blocking collectives  39.5 us
  transfers between devices with their start and end apart: 22, of which 10 were waited for; matrix products, arithmetic and copies ran while one was open for 25% of the time, Pallas kernels for 0%

commit v1 on v0

v1 whole, which is shorter than its diff:
```python
import functools
import math
import jax
import jax.numpy as jnp
from jax import lax
from jax.experimental import pallas as pl
from jax.experimental.layout import Layout, with_layout_constraint
from jax.experimental.pallas import tpu as pltpu
from jax.sharding import PartitionSpec as P

NORM_EPS = 1e-5
ROPE_THETA = 500000.0
ROPE_FACTOR = 8.0
LOW_FACTOR = 1.0
HIGH_FACTOR = 4.0
OLD_CONTEXT = 8192.0
F32 = jnp.float32
BF16 = jnp.bfloat16
D, HEADS, KV, HD, FF = 960, 15, 5, 64, 2560
GROUP = HEADS // KV
BLK = 256
TOKEN_SPEC = P(('dp', 'fsdp'), None, None)
WEIGHT_SPECS = (P(None, 'fsdp'), P(None, 'fsdp', None, None), P(None, 'fsdp', None, None), P(None, 'fsdp', None, None), P(None, 'fsdp', None), P(None, 'fsdp'), P(None, 'fsdp', None), P(None, 'fsdp', None), P(None, 'fsdp', None))
CORE_SWAP = [(i, i ^ 1) for i in range(8)]
DP_SWAP = [(0, 1), (1, 0)]
SAME_CORE = [[0, 2, 4, 6], [1, 3, 5, 7]]
LOG2E = 1.4426950408889634
SCALE = HD ** -0.5


def rope_tables(seq_len, head_dim):
    half_dim = head_dim // 2
    base_freq = 1.0 / (ROPE_THETA ** (jnp.arange(half_dim, dtype=jnp.float32) * 2.0 / head_dim))
    wave_len = 2.0 * math.pi / base_freq
    smooth = (OLD_CONTEXT / wave_len - LOW_FACTOR) / (HIGH_FACTOR - LOW_FACTOR)
    mid_freq = (1.0 - smooth) * base_freq / ROPE_FACTOR + smooth * base_freq
    scaled_freq = jnp.where(wave_len < OLD_CONTEXT / HIGH_FACTOR, base_freq, jnp.where(wave_len > OLD_CONTEXT / LOW_FACTOR, base_freq / ROPE_FACTOR, mid_freq))
    angles = jnp.arange(seq_len, dtype=jnp.float32)[None, :] * scaled_freq[:, None]
    return jnp.cos(angles), jnp.sin(angles)


def dot_nn(a, b):
    return lax.dot_general(a, b, (((1,), (0,)), ((), ())), preferred_element_type=F32)


def dot_nt(a, b):
    return lax.dot_general(a, b, (((1,), (1,)), ((), ())), preferred_element_type=F32)


def dot_tn(a, b):
    return lax.dot_general(a, b, (((0,), (0,)), ((), ())), preferred_element_type=F32)


def rotate(x, cos, sin):
    u, w = x[:HD // 2], x[HD // 2:]
    return jnp.concatenate([u * cos - w * sin, w * cos + u * sin], axis=0)


def unrotate(x, cos, sin):
    u, w = x[:HD // 2], x[HD // 2:]
    return jnp.concatenate([u * cos + w * sin, w * cos - u * sin], axis=0)


def score_parts(k_ref, q, i):
    parts = []
    if i:
        parts.append(dot_nn(k_ref[:i * BLK], q))
    diag = dot_nn(k_ref[i * BLK:(i + 1) * BLK], q)
    keys = lax.broadcasted_iota(jnp.int32, (BLK, BLK), 0)
    queries = lax.broadcasted_iota(jnp.int32, (BLK, BLK), 1)
    parts.append(jnp.where(keys <= queries, diag, -1e30 / SCALE))
    return parts


def softmax_parts(parts):
    top = functools.reduce(jnp.maximum, [jnp.max(s, axis=0, keepdims=True) for s in parts])
    exps = [jnp.exp2((s - top) * (SCALE * LOG2E)) for s in parts]
    inv = 1.0 / sum(jnp.sum(e, axis=0, keepdims=True) for e in exps)
    return [e * inv for e in exps]


def attn_fwd_kernel(q_ref, k_ref, v_ref, cos_ref, sin_ref, qr_ref, kr_ref, vb_ref, o_ref, kt_ref):
    cos, sin = cos_ref[...], sin_ref[...]
    kr = rotate(k_ref[...], cos, sin).astype(BF16)
    kr_ref[...] = kr
    kt_ref[...] = jnp.transpose(kr.astype(F32)).astype(BF16)
    vb_ref[...] = v_ref[...].astype(BF16)

    def head(h, carry):
        rows = pl.ds(pl.multiple_of(h * HD, HD), HD)
        qr_ref[rows, :] = rotate(q_ref[rows, :], cos, sin).astype(BF16)
        for i in range(q_ref.shape[1] // BLK):
            cols = slice(i * BLK, (i + 1) * BLK)
            probs = softmax_parts(score_parts(kt_ref, qr_ref[rows, cols], i))
            base = 0
            out = None
            for p in probs:
                term = dot_nn(vb_ref[:, base:base + p.shape[0]], p.astype(BF16))
                out = term if out is None else out + term
                base += p.shape[0]
            o_ref[rows, cols] = out.astype(BF16)
        return carry

    lax.fori_loop(0, GROUP, head, 0)


def attn_bwd_kernel(q_ref, k_ref, v_ref, do_ref, cos_ref, sin_ref, dq_ref, dk_ref, dv_ref, kt_ref, vt_ref, dka_ref, dva_ref):
    cos, sin = cos_ref[...], sin_ref[...]
    kt_ref[...] = jnp.transpose(k_ref[...].astype(F32)).astype(BF16)
    vt_ref[...] = jnp.transpose(v_ref[...].astype(F32)).astype(BF16)
    dka_ref[...] = jnp.zeros_like(dka_ref)
    dva_ref[...] = jnp.zeros_like(dva_ref)

    def head(h, carry):
        rows = pl.ds(pl.multiple_of(h * HD, HD), HD)
        for i in range(q_ref.shape[1] // BLK):
            cols = slice(i * BLK, (i + 1) * BLK)
            q, do = q_ref[rows, cols], do_ref[rows, cols]
            probs = softmax_parts(score_parts(kt_ref, q, i))
            base = 0
            dps = []
            for p in probs:
                keys = slice(base, base + p.shape[0])
                dps.append(dot_nn(vt_ref[keys], do).astype(BF16).astype(F32))
                dva_ref[keys] += dot_nt(p.astype(BF16), do)
                base += p.shape[0]
            mean = sum(jnp.sum(p * dp, axis=0, keepdims=True) for p, dp in zip(probs, dps))
            base = 0
            dq = None
            for p, dp in zip(probs, dps):
                keys = slice(base, base + p.shape[0])
                ds = (p * (dp - mean)).astype(BF16)
                dka_ref[keys] += dot_nt(ds, q)
                term = dot_nn(k_ref[:, keys], ds)
                dq = term if dq is None else dq + term
                base += p.shape[0]
            dq = (dq * SCALE).astype(BF16).astype(F32)
            dq_ref[rows, cols] = unrotate(dq, cos[:, cols], sin[:, cols]).astype(BF16)
        return carry

    lax.fori_loop(0, GROUP, head, 0)
    dk = (jnp.transpose(dka_ref[...]) * SCALE).astype(BF16).astype(F32)
    dk_ref[...] = unrotate(dk, cos, sin).astype(BF16)
    dv_ref[...] = jnp.transpose(dva_ref[...]).astype(BF16)


def head_spec(seq, first, size):
    return pl.BlockSpec((size, seq), lambda g: (first + g, 0))


def attention_forward(qkv, cos, sin):
    seq = qkv.shape[1]
    full = pl.BlockSpec((HD // 2, seq), lambda g: (0, 0))
    shape = lambda rows: jax.ShapeDtypeStruct((rows, seq), BF16)
    return pl.pallas_call(
        attn_fwd_kernel,
        grid=(KV,),
        in_specs=[head_spec(seq, 0, GROUP * HD), head_spec(seq, HEADS, HD), head_spec(seq, HEADS + KV, HD), full, full],
        out_specs=[head_spec(seq, 0, GROUP * HD), head_spec(seq, 0, HD), head_spec(seq, 0, HD), head_spec(seq, 0, GROUP * HD)],
        out_shape=[shape(HEADS * HD), shape(KV * HD), shape(KV * HD), shape(HEADS * HD)],
        scratch_shapes=[pltpu.VMEM((seq, HD), BF16)],
        compiler_params=pltpu.CompilerParams(dimension_semantics=('arbitrary',), vmem_limit_bytes=48 * 1024 * 1024),
        cost_estimate=pl.CostEstimate(flops=20_000_000_000, bytes_accessed=14_000_000, transcendentals=10_000_000),
        name='attn_fwd',
    )(qkv, qkv, qkv, cos, sin)


def attention_backward(qr, kr, vb, do, cos, sin):
    seq = qr.shape[1]
    full = pl.BlockSpec((HD // 2, seq), lambda g: (0, 0))
    shape = lambda rows: jax.ShapeDtypeStruct((rows, seq), BF16)
    return pl.pallas_call(
        attn_bwd_kernel,
        grid=(KV,),
        in_specs=[head_spec(seq, 0, GROUP * HD), head_spec(seq, 0, HD), head_spec(seq, 0, HD), head_spec(seq, 0, GROUP * HD), full, full],
        out_specs=[head_spec(seq, 0, GROUP * HD), head_spec(seq, 0, HD), head_spec(seq, 0, HD)],
        out_shape=[shape(HEADS * HD), shape(KV * HD), shape(KV * HD)],
        scratch_shapes=[pltpu.VMEM((seq, HD), BF16), pltpu.VMEM((seq, HD), BF16), pltpu.VMEM((seq, HD), F32), pltpu.VMEM((seq, HD), F32)],
        compiler_params=pltpu.CompilerParams(dimension_semantics=('arbitrary',), vmem_limit_bytes=48 * 1024 * 1024),
        cost_estimate=pl.CostEstimate(flops=40_000_000_000, bytes_accessed=14_000_000, transcendentals=10_000_000),
        name='attn_bwd',
    )(qr, kr, vb, do, cos, sin)


def mlp_bwd_kernel(down_ref, grad_ref, gate_ref, up_ref, out_ref):
    dact = dot_nn(down_ref[...], grad_ref[...]).astype(BF16).astype(F32)
    gate, up = gate_ref[...], up_ref[...]
    sig = jax.nn.sigmoid(gate)
    out_ref[0] = (dact * up * (sig * (1.0 + gate * (1.0 - sig)))).astype(BF16)
    out_ref[1] = (dact * (gate * sig)).astype(BF16)


def mlp_backward(down, grad, gate, up):
    seq = grad.shape[1]
    rows = pl.BlockSpec((256, seq), lambda i: (i, 0))
    out = pl.pallas_call(
        mlp_bwd_kernel,
        grid=(FF // 256,),
        in_specs=[pl.BlockSpec((256, D), lambda i: (i, 0)), pl.BlockSpec((D, seq), lambda i: (0, 0)), rows, rows],
        out_specs=pl.BlockSpec((2, 256, seq), lambda i: (0, i, 0)),
        out_shape=jax.ShapeDtypeStruct((2, FF, seq), BF16),
        compiler_params=pltpu.CompilerParams(dimension_semantics=('arbitrary',), vmem_limit_bytes=32 * 1024 * 1024),
        cost_estimate=pl.CostEstimate(flops=5_000_000_000, bytes_accessed=38_000_000, transcendentals=5_000_000),
        name='mlp_bwd',
    )(down, grad, gate, up)
    return out.reshape(2 * FF, seq)


def rms_forward(x, gain):
    inv = lax.rsqrt(jnp.mean(x * x, axis=0, keepdims=True) + NORM_EPS)
    return (x * inv * gain).astype(BF16), inv


def rms_backward(x, inv, gain, dn):
    dgain = jnp.sum(dn * (x * inv), axis=1)
    dxn = dn * gain
    dot = jnp.sum(dxn * x, axis=0, keepdims=True)
    return dxn * inv - x * (inv * inv * inv * dot * (1.0 / x.shape[0])), dgain


def core_half(a, core):
    rows = a.shape[0] // 8
    blocks = a.reshape(4, 2, rows, a.shape[1])
    return lax.dynamic_index_in_dim(blocks, core, axis=1, keepdims=False).reshape(4 * rows, a.shape[1])


def to_peer(part):
    return lax.ppermute(part, 'fsdp', CORE_SWAP)


def row_major(a):
    return with_layout_constraint(a, Layout(major_to_minor=(0, 1)))


def over_chips(part):
    return lax.psum_scatter(part, 'fsdp', scatter_dimension=0, tiled=True, axis_index_groups=SAME_CORE)


def over_dp(mine):
    peer = lax.ppermute(mine, 'dp', DP_SWAP)
    return mine + peer


def tie(*values):
    return lax.optimization_barrier(values)


def gather(shard):
    return lax.all_gather(shard, 'fsdp', axis=0, tiled=True)


def solution(mesh):
    device_count = mesh.shape['dp'] * mesh.shape['fsdp']

    def local_step(hidden, cot_out, attn_norm, w_query, w_key, w_value, w_out, mlp_norm, w_gate, w_up, w_down):
        layers = attn_norm.shape[0]
        rows = attn_norm.shape[1]
        seq = hidden.shape[1]
        core = lax.rem(lax.axis_index('fsdp'), 2)
        cos, sin = rope_tables(seq, HD)
        grad_scale = 1.0 / (seq * device_count)
        gains = jnp.stack([attn_norm[0], mlp_norm[0], attn_norm[1], mlp_norm[1]], axis=1)
        gains = jnp.pad(gains, ((0, 0), (0, 124)))
        weights = []
        for l in range(layers):
            pieces = [w_query[l].reshape(rows, HEADS * HD), w_key[l].reshape(rows, KV * HD), w_value[l].reshape(rows, KV * HD), w_out[l]]
            if l == 0:
                pieces.append(gains)
            attn_w = gather(jnp.concatenate(pieces, axis=1))
            gate_up = gather(jnp.concatenate([w_gate[l], w_up[l]], axis=1))
            down = gather(w_down[l])
            weights.append((attn_w, gate_up, down))
        gain_cols = weights[0][0][:, 2560:2564].astype(F32)
        x = hidden[0].T
        saved = []
        for l in range(layers):
            attn_w, gate_up, down = weights[l]
            g1, g2 = gain_cols[:, 2 * l:2 * l + 1], gain_cols[:, 2 * l + 1:2 * l + 2]
            xf = x.astype(F32)
            a, inv1 = rms_forward(xf, g1)
            qkv = dot_tn(attn_w[:, :1600], a)
            qr, kr, vb, o = attention_forward(qkv, cos, sin)
            x1 = (xf + dot_tn(attn_w[:, 1600:2560], o)).astype(BF16)
            x1f = x1.astype(F32)
            b, inv2 = rms_forward(x1f, g2)
            gate = dot_tn(gate_up[:, :FF], b)
            up = dot_tn(gate_up[:, FF:], b)
            act = (jax.nn.silu(gate) * up).astype(BF16)
            saved.append((x, a, inv1, g1, qr, kr, vb, o, x1, b, inv2, g2, gate, up, act))
            x = (x1f + dot_tn(down, act)).astype(BF16)
        y = x
        grad = cot_out[0].T
        outs = [[None] * 3 for _ in range(layers)]
        gain_grads = [None] * (2 * layers)
        waiting = []

        def release(value):
            if not waiting:
                return value
            l, slot, part = waiting.pop(0)
            value, part = tie(value, part)
            outs[l][slot] = over_dp(part)
            return value

        for l in reversed(range(layers)):
            attn_w, gate_up, down = weights[l]
            x, a, inv1, g1, qr, kr, vb, o, x1, b, inv2, g2, gate, up, act = saved[l]
            wide = jnp.pad(grad, ((0, 64), (0, 0)))
            other_down = row_major(dot_nt(core_half(act, 1 - core), wide))
            grad, other_down = tie(grad, other_down)
            sent_down = to_peer(other_down)
            dgu = mlp_backward(down, grad, gate, up)
            act_mine, dgu = tie(core_half(act, core), dgu)
            mine_down = row_major(dot_nt(act_mine, wide) + sent_down)
            other_gu = row_major(dot_nt(core_half(b, 1 - core), dgu))
            dgu, mine_down, other_gu = tie(dgu, mine_down, other_gu)
            waiting.append((l, 2, over_chips(mine_down)))
            sent_gu = to_peer(other_gu)
            db = dot_nn(gate_up, dgu).astype(BF16).astype(F32)
            dx1n, gain_grads[2 * l + 1] = rms_backward(x1.astype(F32), inv2, g2, db)
            dmid = (grad.astype(F32) + dx1n).astype(BF16)
            if l == 0:
                dmid = release(dmid)
            b_mine, dmid = tie(core_half(b, core), dmid)
            mine_gu = row_major(dot_nt(b_mine, dgu) + sent_gu)
            other_o = row_major(dot_nt(core_half(o, 1 - core), dmid))
            dmid, mine_gu, other_o = tie(dmid, mine_gu, other_o)
            waiting.append((l, 1, over_chips(mine_gu)))
            sent_o = to_peer(other_o)
            do = dot_nn(attn_w[:, 1600:2560], dmid).astype(BF16)
            dq, dk, dv = attention_backward(qr, kr, vb, do, cos, sin)
            dqkv = release(jnp.concatenate([dq, dk, dv], axis=0))
            o_mine, dqkv = tie(core_half(o, core), dqkv)
            mine_o = dot_nt(o_mine, dmid) + sent_o
            other_qkv = row_major(dot_nt(core_half(a, 1 - core), dqkv))
            dqkv, mine_o, other_qkv = tie(dqkv, mine_o, other_qkv)
            sent_qkv = to_peer(other_qkv)
            da = dot_nn(attn_w[:, :1600], dqkv).astype(BF16).astype(F32)
            dxn, gain_grads[2 * l] = rms_backward(x.astype(F32), inv1, g1, da)
            grad = (dmid.astype(F32) + dxn).astype(BF16)
            a_mine, grad = tie(core_half(a, core), grad)
            parts = [dot_nt(a_mine, dqkv) + sent_qkv, mine_o]
            if l == 0:
                cols = jnp.pad(jnp.stack(gain_grads, axis=1), ((0, 0), (0, 124)))
                parts.append(core_half(cols, core) + to_peer(core_half(cols, 1 - core)))
            part = row_major(jnp.concatenate(parts, axis=1))
            grad, part = tie(grad, part)
            if l == 0:
                part = release(release(part))
            waiting.append((l, 0, over_chips(part)))
        for l, slot, part in waiting:
            outs[l][slot] = over_dp(part)
        ra = [o[0] * grad_scale for o in outs]
        rg = [o[1] * grad_scale for o in outs]
        rd = [o[2][:, :D] * grad_scale for o in outs]
        gain = ra[0][:, 2560:2564]
        stack = lambda parts: jnp.stack(parts)
        return (
            y.T[None], grad.T[None],
            stack([gain[:, 0], gain[:, 2]]),
            stack([r[:, :960].reshape(rows, HEADS, HD) for r in ra]),
            stack([r[:, 960:1280].reshape(rows, KV, HD) for r in ra]),
            stack([r[:, 1280:1600].reshape(rows, KV, HD) for r in ra]),
            stack([r[:, 1600:2560] for r in ra]),
            stack([gain[:, 1], gain[:, 3]]),
            stack([r[:, :FF] for r in rg]),
            stack([r[:, FF:] for r in rg]),
            stack(rd),
        )

    return jax.shard_map(local_step, mesh=mesh, in_specs=(TOKEN_SPEC, TOKEN_SPEC) + WEIGHT_SPECS, out_specs=(TOKEN_SPEC, TOKEN_SPEC) + WEIGHT_SPECS, check_vma=False)
```

time: 1740 us -> 947 us (0.54)
  matrix products: 658 us -> 235 us
  waiting for transfers between devices: 790 us -> 387 us
  Pallas kernels: 0 us -> 177 us
  blocking collectives: 124 us -> 0 us
  other arithmetic: 82.7 us -> 42.6 us
    reduce_scatter x8 -> x2, waiting for transfers between devices: 559 us -> 0.02 us  [over_chips(): lax.psum_scatter(part, 'fsdp', scatter_dimension=0, tiled=True, axis_inde...]
    dot_general x42 -> x32, matrix products: 622 us -> 235 us  [the longest x10 94 us: dot_tn(): lax.dot_general(a, b, (((0,), (0,)), ((), ())), preferred_element_type=F32)]
    ppermute x0 -> x15, waiting for transfers between devices: none -> 188 us  [the longest x6 188 us: over_dp(): peer = lax.ppermute(mine, 'dp', DP_SWAP)]
    psum x1 -> x0, waiting for transfers between devices: 184 us -> none  [local_step(): lax.psum(lax.psum_scatter(local_grad, 'fsdp', scatter_dimension=0, tiled=...]
    pallas_call x0 -> x6, Pallas kernels: none -> 177 us  [the longest x2 89.7 us: attention_backward(): pl.pallas_call(attn_bwd_kernel, grid=(KV,), in_specs=[head_spec(seq, 0, G...]
    all_gather x10 -> x6, waiting for transfers between devices: 0.04 us -> 105 us  [gather(): return lax.all_gather(shard, 'fsdp', axis=0, tiled=True)]
    optimization_barrier x0 -> x3, waiting for transfers between devices: none -> 92.9 us  [tie(): return lax.optimization_barrier(values)]
    all_gather x4 -> x0, blocking collectives: 79 us -> none  [local_step(): lax.all_gather(weight_shard[layer_idx], 'fsdp', axis=0, tiled=True)]
  transfers between devices with their start and end apart: 22 -> 27, of which waited for: 10 -> 12; matrix products, arithmetic and copies ran while one was open for 25% -> 33% of each run, Pallas kernels for 0% -> 19%
where the time goes in v1:
time: 947 us; the launch traced here: 936 us
  waiting for transfers between devices  387 us (41%)
  matrix products  235 us (25%)
  Pallas kernels  177 us (19%)
  local copies, waits for them, and re-layouts  68.1 us (7%)
  other arithmetic  42.6 us (4%)
  between operations  15.9 us (2%)
  starting transfers between devices  10.1 us (1%)
    ppermute x6, waiting for transfers between devices, over_dp(): peer = lax.ppermute(mine, 'dp', DP_SWAP)  188 us
    all_gather x6, waiting for transfers between devices, gather(): return lax.all_gather(shard, 'fsdp', axis=0, tiled=True)  105 us
    dot_general x10, matrix products, dot_tn(): lax.dot_general(a, b, (((0,), (0,)), ((), ())), preferred_element_type=F32)  94 us
    optimization_barrier x3, waiting for transfers between devices, tie(): return lax.optimization_barrier(values)  92.9 us
    pallas_call x2, Pallas kernels, attention_backward(): pl.pallas_call(attn_bwd_kernel, grid=(KV,), in_specs=[head_spec(seq, 0, G...  89.7 us
    dot_general x16, matrix products, dot_nt(): lax.dot_general(a, b, (((1,), (1,)), ((), ())), preferred_element_type=F32)  85.2 us
    pallas_call x2, Pallas kernels, attention_forward(): pl.pallas_call(attn_fwd_kernel, grid=(KV,), in_specs=[head_spec(seq, 0, G...  58.6 us
    dot_general x6, matrix products, dot_nn(): lax.dot_general(a, b, (((1,), (0,)), ((), ())), preferred_element_type=F32)  56.3 us
  transfers between devices with their start and end apart: 27, of which 12 were waited for; matrix products, arithmetic and copies ran while one was open for 33% of the time, Pallas kernels for 19%

profile of v1, /device:TPU:0, one launch (start us, length us, event | category | flops | bytes accessed | tf_op | source)
XLA Modules:
  0.0 935.8 jit_solution(1219807938028302775)
XLA Ops:
  25.9 28.8 %all-gather.9.cloned.1.call-done = bf16[960,2688]{1,0:T(8,128)(2,1)} async-done(((bf16[120,2688]{1,0:T(8,128)(2,1)}), bf16[960,2688]{1,0:T(8,128)(2,1)}) %all-gather.9.cloned.1.call-update) | async-done | bytes 5160976 | tf_op jit(solution)/shard_map/all_gather | solution.py:249
  58.0 5.6 fusion.60.q_ref.k_ref.v_ref
  63.6 29.0 %attn_fwd.2 = (bf16[960,1024]{1,0:T(8,128)(2,1)S(1)}, bf16[320,1024]{1,0:T(8,128)(2,1)S(1)}, bf16[320,1024]{1,0:T(8,128)(2,1)S(1)}, bf16[960,1024]{1,0:T(8,128)(2,1)S(1)}) custom-call(f32[1600,1024]{1,0:T(8,128)} %fusion.60.q_ref.k_ref.v_ref, f32[1600,1024]{1,0:T(8,128)} %fusion.60.q_ref.k_ref.v_ref, f32[1600,1024]{1,0:T(8,128)} %fusion.60.q_ref.k_ref.v_ref, ...), custom_call_target="tpu_custom_call" | custom-call | flops 20000000000 | bytes 14000000 | tf_op jit(solution)/shard_map/attn_fwd/pallas_call | solution.py:155
  92.6 4.7 fusion.47
  99.1 14.8 %all-gather.11.cloned.1.call-done = bf16[960,5120]{1,0:T(8,128)(2,1)} async-done(((bf16[120,5120]{1,0:T(8,128)(2,1)}), bf16[960,5120]{1,0:T(8,128)(2,1)}) %all-gather.11.cloned.1.call-update) | async-done | bytes 9830416 | tf_op jit(solution)/shard_map/all_gather | solution.py:249
  113.8 7.7 fusion.6.gate_ref
  121.5 3.9 copy-done.14
  125.4 13.3 %multiply_convert_fusion.1 = (bf16[2560,1024]{1,0:T(8,128)(2,1)}, f32[2560,1024]{1,0:T(8,128)}) fusion(f32[2560,1024]{1,0:T(8,128)S(1)} %fusion.6.gate_ref, bf16[960,1024]{1,0:T(8,128)(2,1)S(1)} %fusion.22, bf16[960,5120]{1,0:T(8,128)(2,1)} %all-gather.11.cloned.1.call-done), kind=kOutput, calls=%fused_computation.1 | convolution fusion | flops 5048893440 | bytes 33095680 | tf_op jit(solution)/shard_map/dot_general | solution.py:51
  138.8 14.8 %all-gather.17.cloned.1.call-done = bf16[1,2560,960]{2,1,0:T(8,128)(2,1)} async-done(((bf16[1,320,960]{2,1,0:T(8,128)(2,1)}), bf16[1,2560,960]{2,1,0:T(8,128)(2,1)}) %all-gather.17.cloned.1.call-update) | async-done | bytes 4915216 | tf_op jit(solution)/shard_map/all_gather | solution.py:249
  153.6 10.5 %fusion.50 = (f32[1024]{0:T(1024)S(1)}, bf16[960,1024]{1,0:T(8,128)(2,1)S(1)}, f32[1024,960]{0,1:T(8,128)}) fusion(bf16[960,1024]{1,0:T(8,128)(2,1)} %copy-done.24, bf16[2560,1024]{1,0:T(8,128)(2,1)} %get-tuple-element.238, bf16[1,2560,960]{2,1,0:T(8,128)(2,1)} %all-gather.17.cloned.1.call-done), kind=kOutput, calls=%fused_computation.81 | convolution fusion | flops 5039062016 | bytes 18026496 | tf_op jit(solution)/shard_map/dot_general | solution.py:51
  165.9 25.9 %all-gather.13.cloned.1.call-done = bf16[960,2560]{1,0:T(8,128)(2,1)} async-done(((bf16[120,2560]{1,0:T(8,128)(2,1)}), bf16[960,2560]{1,0:T(8,128)(2,1)}) %all-gather.13.cloned.1.call-update) | async-done | bytes 4915216 | tf_op jit(solution)/shard_map/all_gather | solution.py:249
  191.8 7.5 fusion.56.q_ref.k_ref.v_ref
  199.3 29.6 %attn_fwd.3 = (bf16[960,1024]{1,0:T(8,128)(2,1)S(1)}, bf16[320,1024]{1,0:T(8,128)(2,1)S(1)}, bf16[320,1024]{1,0:T(8,128)(2,1)S(1)}, bf16[960,1024]{1,0:T(8,128)(2,1)S(1)}) custom-call(f32[1600,1024]{1,0:T(8,128)} %fusion.56.q_ref.k_ref.v_ref, f32[1600,1024]{1,0:T(8,128)} %fusion.56.q_ref.k_ref.v_ref, f32[1600,1024]{1,0:T(8,128)} %fusion.56.q_ref.k_ref.v_ref, ...), custom_call_target="tpu_custom_call" | custom-call | flops 20000000000 | bytes 14000000 | tf_op jit(solution)/shard_map/attn_fwd/pallas_call | solution.py:155
  228.9 7.7 fusion.45
  238.4 12.2 %all-gather.15.cloned.1.call-done = bf16[960,5120]{1,0:T(8,128)(2,1)} async-done(((bf16[120,5120]{1,0:T(8,128)(2,1)}), bf16[960,5120]{1,0:T(8,128)(2,1)}) %all-gather.15.cloned.1.call-update) | async-done | bytes 9830416 | tf_op jit(solution)/shard_map/all_gather | solution.py:249
  250.7 7.7 fusion.2.gate_ref
  258.4 15.9 %multiply_convert_fusion = (bf16[2560,1024]{1,0:T(8,128)(2,1)S(1)}, f32[2560,1024]{1,0:T(8,128)}) fusion(f32[2560,1024]{1,0:T(8,128)S(1)} %fusion.2.gate_ref, bf16[960,1024]{1,0:T(8,128)(2,1)S(1)} %fusion.23, bf16[960,5120]{1,0:T(8,128)(2,1)} %all-gather.15.cloned.1.call-done), kind=kOutput, calls=%fused_computation | convolution fusion | flops 5048893440 | bytes 33095680 | tf_op jit(solution)/shard_map/dot_general | solution.py:51
  277.5 4.7 fusion.67
  282.5 8.1 all-gather.19.cloned.1.call-done
  293.1 14.3 %mlp_bwd.2 = bf16[2,2560,1024]{2,1,0:T(8,128)(2,1)S(1)} custom-call(bf16[2560,960]{1,0:T(8,128)(2,1)S(1)} %bitcast.216, bf16[960,1024]{1,0:T(8,128)(2,1)S(1)} %bitcast.213, f32[2560,1024]{1,0:T(8,128)} %copy-done.15, f32[2560,1024]{1,0:T(8,128)} %get-tuple-element.243.up_ref), custom_call_target="tpu_custom_call" | custom-call | flops 5000000000 | bytes 38000000 | tf_op jit(solution)/shard_map/mlp_bwd/pallas_call | solution.py:196
  308.7 7.7 fusion.120
  316.5 6.5 convolution_add_fusion.3
  326.1 18.3 %fusion.37 = (f32[960]{0:T(1024)}, f32[1024]{0:T(1024)S(1)}, bf16[960,1024]{1,0:T(8,128)(2,1)S(1)}) fusion(bf16[960,1024]{1,0:T(8,128)(2,1)S(1)} %copy-done.30, f32[1024]{0:T(1024)S(1)} %add_rsqrt_fusion, f32[960]{0:T(1024)S(1)} %get-tuple-element.173, bf16[960,5120]{1,0:T(8,128)(2,1)} %all-gather.15.cloned.1.call-done, bf16[5120,1024]{1,0:T(8,128)(2,1)} %bitcast.208), kind=kOutput, calls=%fused_computation.68 | convolution fusion | flops 10075174912 | bytes 24264192 | tf_op jit(solution)/shard_map/dot_general | solution.py:43
  348.2 10.3 %convolution_add_fusion.1 = f32[480,5120]{1,0:T(8,128)} fusion(f32[480,5120]{1,0:T(8,128)} %collective-permute-done.1, bf16[480,1024]{1,0:T(8,128)(2,1)S(1)} %bitcast.243, bf16[5120,1024]{1,0:T(8,128)(2,1)S(1)} %bitcast.211), kind=kOutput, calls=%fused_computation.13 | convolution fusion | flops 5035622400 | bytes 31129600 | tf_op jit(solution)/shard_map/dot_general | solution.py:47
  361.7 5.4 convolution_convert_fusion.3.do_ref
  367.2 44.7 %attn_bwd.2 = (bf16[960,1024]{1,0:T(8,128)(2,1)S(1)}, bf16[320,1024]{1,0:T(8,128)(2,1)S(1)}, bf16[320,1024]{1,0:T(8,128)(2,1)S(1)}) custom-call(bf16[960,1024]{1,0:T(8,128)(2,1)} %copy-done.7, bf16[320,1024]{1,0:T(8,128)(2,1)S(1)} %copy-done.9, bf16[320,1024]{1,0:T(8,128)(2,1)S(1)} %copy-done.11, bf16[960,1024]{1,0:T(8,128)(2,1)} %convolution_convert_fusion.3.do_ref, ...), custom_call_target="tpu_custom_call" | custom-call | flops 40000000000 | bytes 14000000 | tf_op jit(solution)/shard_map/attn_bwd/pallas_call | solution.py:172
  421.7 4.9 fusion.38
  436.4 5.2 fusion.64
  443.2 14.6 %mlp_bwd.3 = bf16[2,2560,1024]{2,1,0:T(8,128)(2,1)S(1)} custom-call(bf16[2560,960]{1,0:T(8,128)(2,1)S(1)} %bitcast.219, bf16[960,1024]{1,0:T(8,128)(2,1)S(1)} %fusion.33.grad_ref, f32[2560,1024]{1,0:T(8,128)} %copy-done.14, f32[2560,1024]{1,0:T(8,128)} %get-tuple-element.239.up_ref), custom_call_target="tpu_custom_call" | custom-call | flops 5000000000 | bytes 38000000 | tf_op jit(solution)/shard_map/mlp_bwd/pallas_call | solution.py:196
  457.8 7.8 fusion.124
  465.6 4.7 convolution_add_fusion.2
  473.6 16.9 %fusion.39 = (f32[960]{0:T(1024)S(1)}, f32[1024]{0:T(1024)S(1)}, bf16[960,1024]{1,0:T(8,128)(2,1)S(1)}) fusion(bf16[960,1024]{1,0:T(8,128)(2,1)S(1)} %copy-done.25, f32[1024]{0:T(1024)S(1)} %copy-done.75, f32[960]{0:T(1024)S(1)} %copy-done.69, bf16[960,5120]{1,0:T(8,128)(2,1)} %all-gather.11.cloned.1.call-done, bf16[5120,1024]{1,0:T(8,128)(2,1)} %bitcast.205), kind=kOutput, calls=%fused_computation.70 | convolution fusion | flops 10075174912 | bytes 24264192 | tf_op jit(solution)/shard_map/dot_general | solution.py:43
  493.0 4.5 fusion.125
  497.5 13.9 %convolution_add_fusion = f32[480,5120]{1,0:T(8,128)} fusion(f32[480,5120]{1,0:T(8,128)} %collective-permute-done.5, bf16[480,1024]{1,0:T(8,128)(2,1)S(1)} %bitcast.242, bf16[5120,1024]{1,0:T(8,128)(2,1)} %bitcast.206), kind=kOutput, calls=%fused_computation.12 | convolution fusion | flops 5035622400 | bytes 31129600 | tf_op jit(solution)/shard_map/dot_general | solution.py:47
  515.1 5.3 convolution_convert_fusion.2.do_ref
  520.4 44.9 %attn_bwd.3 = (bf16[960,1024]{1,0:T(8,128)(2,1)S(1)}, bf16[320,1024]{1,0:T(8,128)(2,1)S(1)}, bf16[320,1024]{1,0:T(8,128)(2,1)S(1)}) custom-call(bf16[960,1024]{1,0:T(8,128)(2,1)} %copy-done.6, bf16[320,1024]{1,0:T(8,128)(2,1)S(1)} %get-tuple-element.117.k_ref, bf16[320,1024]{1,0:T(8,128)(2,1)S(1)} %get-tuple-element.118.v_ref, ...), custom_call_target="tpu_custom_call" | custom-call | flops 40000000000 | bytes 14000000 | tf_op jit(solution)/shard_map/attn_bwd/pallas_call | solution.py:172
  570.5 3.7 fusion.127
  577.7 5.4 fusion.40
  584.9 4.2 fusion.27
  589.2 5.7 convolution_add_fusion.4
  594.9 6.5 concatenate.31
  601.4 92.9 %reduce-scatter.23.cloned.1.call-done = f32[120,5120]{1,0:T(8,128)} async-done(((f32[480,5120]{1,0:T(8,128)}), f32[120,5120]{1,0:T(8,128)}) %reduce-scatter.23.cloned.1.call-update) | async-done | bytes 2457616 | tf_op jit(solution)/shard_map/optimization_barrier | solution.py:245
  697.8 13.4 %fusion.62 = bf16[1,1024,960]{1,2,0:T(8,128)(2,1)} fusion(f32[960,1024]{1,0:T(8,128)} %get-tuple-element.241, f32[1024,960]{0,1:T(8,128)} %get-tuple-element.240, f32[960,1024]{1,0:T(8,128)} %get-tuple-element.237, bf16[1,1024,960]{1,2,0:T(8,128)(2,1)S(1)} %copy-done.13, bf16[2560,1024]{1,0:T(8,128)(2,1)} %copy-done.38, ...), kind=kOutput, calls=%fused_computation.105 | convolution fusion | flops 5044961280 | bytes 25886720 | tf_op jit(solution)/shard_map/dot_general | solution.py:51
  711.2 14.8 %collective-permute-done.14 = f32[320,1024]{1,0:T(8,128)S(1)} collective-permute-done((f32[320,1024]{1,0:T(8,128)S(1)}, f32[320,1024]{1,0:T(8,128)S(1)}, u32[]{:S(2)}, u32[]{:S(2)}) %collective-permute-start.14) | collective-permute-done | bytes 1310752 | tf_op jit(solution)/shard_map/ppermute | solution.py:240
  727.9 75.9 %collective-permute-done.10 = f32[120,2560]{1,0:T(8,128)} collective-permute-done((f32[120,2560]{1,0:T(8,128)}, f32[120,2560]{1,0:T(8,128)}, u32[]{:S(2)}, u32[]{:S(2)}) %collective-permute-start.10) | collective-permute-done | bytes 1228832 | tf_op jit(solution)/shard_map/ppermute | solution.py:240
  815.4 26.0 %collective-permute-done.13 = f32[320,1024]{1,0:T(8,128)S(1)} collective-permute-done((f32[320,1024]{1,0:T(8,128)S(1)}, f32[320,1024]{1,0:T(8,128)S(1)}, u32[]{:S(2)}, u32[]{:S(2)}) %collective-permute-start.13) | collective-permute-done | bytes 1310752 | tf_op jit(solution)/shard_map/ppermute | solution.py:240
  843.3 48.6 %collective-permute-done.11 = f32[120,5120]{1,0:T(8,128)S(1)} collective-permute-done((f32[120,5120]{1,0:T(8,128)S(1)}, f32[120,5120]{1,0:T(8,128)S(1)}, u32[]{:S(2)}, u32[]{:S(2)}) %collective-permute-start.11) | collective-permute-done | bytes 2457632 | tf_op jit(solution)/shard_map/ppermute | solution.py:240
  897.6 23.1 %collective-permute-done.9 = f32[120,2688]{1,0:T(8,128)} collective-permute-done((f32[120,2688]{1,0:T(8,128)}, f32[120,2688]{1,0:T(8,128)}, u32[]{:S(2)}, u32[]{:S(2)}) %collective-permute-start.9) | collective-permute-done | bytes 1290272 | tf_op jit(solution)/shard_map/ppermute | solution.py:240
  (338 shorter events, 117.4 us)
Async XLA Ops:
  7.2 47.5 %all-gather.9.cloned.1.call-start = ((), (), s32[]{:S(2)}) async-start(), calls=%async_computation.6 | async-start | bytes 5806080 | tf_op jit(solution)/shard_map/all_gather | solution.py:249
  14.9 98.9 %all-gather.11.cloned.1.call-start = ((), (), s32[]{:S(2)}) async-start(), calls=%async_computation.7 | async-start | bytes 11059200 | tf_op jit(solution)/shard_map/all_gather | solution.py:249
  18.5 135.1 %all-gather.17.cloned.1.call-start = ((), (), s32[]{:S(2)}) async-start(), calls=%async_computation.12 | async-start | bytes 5898240 | tf_op jit(solution)/shard_map/all_gather | solution.py:249
  19.8 172.0 %all-gather.13.cloned.1.call-start = ((), (), s32[]{:S(2)}) async-start(), calls=%async_computation.8 | async-start | bytes 5529600 | tf_op jit(solution)/shard_map/all_gather | solution.py:249
  21.3 229.4 %all-gather.15.cloned.1.call-start = ((), (), s32[]{:S(2)}) async-start(), calls=%async_computation.9 | async-start | bytes 11059200 | tf_op jit(solution)/shard_map/all_gather | solution.py:249
  23.6 266.9 %all-gather.19.cloned.1.call-start = ((), (), s32[]{:S(2)}) async-start(), calls=%async_computation.13 | async-start | bytes 5898240 | tf_op jit(solution)/shard_map/all_gather | solution.py:249
  24.2 389.9 %reduce-scatter.15.cloned.1.call-start = ((), (), s32[]{:S(2)}) async-start(), calls=%async_computation.10 | async-start | bytes 6553600 | tf_op jit(solution)/shard_map/reduce_scatter | solution.py:236
  25.3 32.6 %copy-start.72 = (f32[1024]{0:T(1024)}, f32[1024]{0:T(1024)S(1)}, u32[]{:S(2)}) copy-start(f32[1024]{0:T(1024)S(1)} %add_rsqrt_fusion.3) | copy-start | bytes 12292
  56.9 41.0 %copy-start.68 = (f32[960]{0:T(1024)}, f32[960]{0:T(1024)S(1)}, u32[]{:S(2)}) copy-start(f32[960]{0:T(1024)S(1)} %get-tuple-element.175) | copy-start | bytes 11524
  56.9 107.8 %copy-start.70 = (f32[960]{0:T(1024)}, f32[960]{0:T(1024)S(1)}, u32[]{:S(2)}) copy-start(f32[960]{0:T(1024)S(1)} %get-tuple-element.174) | copy-start | bytes 11524
  99.0 22.4 %copy-start.18 = (bf16[960,1024]{1,0:T(8,128)(2,1)}, bf16[960,1024]{1,0:T(8,128)(2,1)S(1)}, u32[]{:S(2)}) copy-start(bf16[960,1024]{1,0:T(8,128)(2,1)S(1)} %fusion.22) | copy-start | bytes 5898244
  165.9 33.3 %copy-start.20 = (bf16[960,1024]{1,0:T(8,128)(2,1)}, bf16[960,1024]{1,0:T(8,128)(2,1)S(1)}, u32[]{:S(2)}) copy-start(bf16[960,1024]{1,0:T(8,128)(2,1)S(1)} %fusion.21) | copy-start | bytes 5898244
  199.3 29.7 %copy-start.27 = (bf16[960,1024]{1,0:T(8,128)(2,1)S(1)}, bf16[960,1024]{1,0:T(8,128)(2,1)}, u32[]{:S(2)}) copy-start(bf16[960,1024]{1,0:T(8,128)(2,1)} %copy-done.26) | copy-start | bytes 5898244
  228.9 7.8 copy-start.5
  228.9 7.8 copy-start.7
  228.9 7.8 copy-start.8
  228.9 7.8 copy-start.10
  238.4 19.9 %copy-start.22 = (bf16[960,1024]{1,0:T(8,128)(2,1)}, bf16[960,1024]{1,0:T(8,128)(2,1)S(1)}, u32[]{:S(2)}) copy-start(bf16[960,1024]{1,0:T(8,128)(2,1)S(1)} %fusion.23) | copy-start | bytes 5898244
  258.3 15.9 %copy-start.15 = (f32[2560,1024]{1,0:T(8,128)}, f32[2560,1024]{1,0:T(8,128)S(1)}, u32[]{:S(2)}) copy-start(f32[2560,1024]{1,0:T(8,128)S(1)} %fusion.2.gate_ref) | copy-start | bytes 31457284
  282.2 34.2 %collective-permute-start = (f32[1280,1024]{1,0:T(8,128)}, f32[1280,1024]{1,0:T(8,128)}, u32[]{:S(2)}, u32[]{:S(2)}) collective-permute-start(f32[1280,1024]{1,0:T(8,128)} %fusion.67), channel_id=1, source_target_pairs={{0,1},{1,0},{2,3},{3,2},{4,5},{5,4},{6,7},{7,6},{8,9},{9,8},{10,11... | collective-permute-start | bytes 15728648 | tf_op jit(solution)/shard_map/ppermute | solution.py:228
  293.1 14.4 %copy-start.23 = (bf16[960,1024]{1,0:T(8,128)(2,1)S(1)}, bf16[960,1024]{1,0:T(8,128)(2,1)}, u32[]{:S(2)}) copy-start(bf16[960,1024]{1,0:T(8,128)(2,1)} %copy-done.22) | copy-start | bytes 5898244
  307.4 9.1 copy-start.1
  323.0 25.1 %collective-permute-start.1 = (f32[480,5120]{1,0:T(8,128)}, f32[480,5120]{1,0:T(8,128)}, u32[]{:S(2)}, u32[]{:S(2)}) collective-permute-start(f32[480,5120]{1,0:T(8,128)} %fusion.120), channel_id=1, source_target_pairs={{0,1},{1,0},{2,3},{3,2},{4,5},{5,4},{6,7},{7,6},{8,9},{9,8},{10,11... | collective-permute-start | bytes 29491208 | tf_op jit(solution)/shard_map/ppermute | solution.py:228
  323.3 169.7 %reduce-scatter.19.cloned.1.call-start = ((), (), s32[]{:S(2)}) async-start(), calls=%async_computation.14 | async-start | bytes 12288000
  323.3 24.8 %slice-start = ((s8[10485760]{0:T(1024)(128)(4,1)}), s8[4194304]{0:T(1024)(128)(4,1)S(1)}, s32[]{:S(2)}) async-start(s8[10485760]{0:T(1024)(128)(4,1)} %bitcast.209), calls=%async_computation.18 | async-start | bytes 8388608
  326.1 22.0 %slice-start.1 = ((s8[10485760]{0:T(1024)(128)(4,1)}), s8[4194304]{0:T(1024)(128)(4,1)S(1)}, s32[]{:S(2)}) async-start(s8[10485760]{0:T(1024)(128)(4,1)} %bitcast.209), calls=%async_computation.19 | async-start | bytes 8388608
  326.1 22.0 %slice-start.2 = ((s8[10485760]{0:T(1024)(128)(4,1)}), s8[2097152]{0:T(1024)(128)(4,1)S(1)}, s32[]{:S(2)}) async-start(s8[10485760]{0:T(1024)(128)(4,1)} %bitcast.209), calls=%async_computation.20 | async-start | bytes 4194304
  358.4 208.9 %reduce-scatter.21.cloned.1.call-start = ((), (), s32[]{:S(2)}) async-start(), calls=%async_computation.15 | async-start | bytes 6144000
  361.5 58.0 %collective-permute-start.2 = (f32[480,960]{1,0:T(8,128)}, f32[480,960]{1,0:T(8,128)}, u32[]{:S(2)}, u32[]{:S(2)}) collective-permute-start(f32[480,960]{1,0:T(8,128)} %fusion.121), channel_id=1, source_target_pairs={{0,1},{1,0},{2,3},{3,2},{4,5},{5,4},{6,7},{7,6},{8,9},{9,8},{10,11... | collective-permute-start | bytes 5529608 | tf_op jit(solution)/shard_map/ppermute | solution.py:228
  421.6 6.2 collective-permute-start.3
  433.1 168.3 %reduce-scatter.17.cloned.1.call-start = ((), (), s32[]{:S(2)}) async-start(), calls=%async_computation.11 | async-start | bytes 6553600 | tf_op jit(solution)/shard_map/reduce_scatter | solution.py:236
  441.5 24.1 %collective-permute-start.4 = (f32[1280,1024]{1,0:T(8,128)}, f32[1280,1024]{1,0:T(8,128)S(1)}, u32[]{:S(2)}, u32[]{:S(2)}) collective-permute-start(f32[1280,1024]{1,0:T(8,128)} %fusion.64), channel_id=1, source_target_pairs={{0,1},{1,0},{2,3},{3,2},{4,5},{5,4},{6,7},{7,6},{8,9},{9,8},{10,11... | collective-permute-start | bytes 15728648 | tf_op jit(solution)/shard_map/ppermute | solution.py:228
  457.8 7.8 copy-start
  470.4 27.1 %collective-permute-start.5 = (f32[480,5120]{1,0:T(8,128)}, f32[480,5120]{1,0:T(8,128)}, u32[]{:S(2)}, u32[]{:S(2)}) collective-permute-start(f32[480,5120]{1,0:T(8,128)} %fusion.124), channel_id=1, source_target_pairs={{0,1},{1,0},{2,3},{3,2},{4,5},{5,4},{6,7},{7,6},{8,9},{9,8},{10,11... | collective-permute-start | bytes 29491208 | tf_op jit(solution)/shard_map/ppermute | solution.py:228
  470.4 223.9 %reduce-scatter.23.cloned.1.call-start = ((), (), s32[]{:S(2)}) async-start(), calls=%async_computation.16 | async-start | bytes 12288000
  473.6 16.9 %copy-start.79 = (f32[1024]{0:T(1024)S(1)}, f32[1024]{0:T(1024)}, u32[]{:S(2)}) copy-start(f32[1024]{0:T(1024)} %copy-done.78) | copy-start | bytes 12292
  511.4 380.7 %reduce-scatter.25.cloned.1.call-start = ((), (), s32[]{:S(2)}) async-start(), calls=%async_computation.17 | async-start | bytes 6451200
  514.4 59.8 %collective-permute-start.6 = (f32[480,960]{1,0:T(8,128)}, f32[480,960]{1,0:T(8,128)}, u32[]{:S(2)}, u32[]{:S(2)}) collective-permute-start(f32[480,960]{1,0:T(8,128)} %fusion.125), channel_id=1, source_target_pairs={{0,1},{1,0},{2,3},{3,2},{4,5},{5,4},{6,7},{7,6},{8,9},{9,8},{10,11... | collective-permute-start | bytes 5529608 | tf_op jit(solution)/shard_map/ppermute | solution.py:228
  568.3 9.3 slice-start.5
  577.6 11.5 %collective-permute-start.7 = (f32[480,1600]{1,0:T(8,128)}, f32[480,1600]{1,0:T(8,128)}, u32[]{:S(2)}, u32[]{:S(2)}) collective-permute-start(f32[480,1600]{1,0:T(8,128)} %fusion.127), channel_id=1, source_target_pairs={{0,1},{1,0},{2,3},{3,2},{4,5},{5,4},{6,7},{7,6},{8,9},{9,8},{10,11... | collective-permute-start | bytes 9216008 | tf_op jit(solution)/shard_map/ppermute | solution.py:228
  583.5 5.6 collective-permute-start.8
  601.4 92.9 %copy-start.49 = (f32[320,1024]{1,0:T(8,128)S(1)}, f32[320,1024]{1,0:T(8,128)}, u32[]{:S(2)}) copy-start(f32[320,1024]{1,0:T(8,128)} %reduce-scatter.15.cloned.1.call-done) | copy-start | bytes 3932164
  694.3 31.7 %collective-permute-start.14 = (f32[320,1024]{1,0:T(8,128)S(1)}, f32[320,1024]{1,0:T(8,128)S(1)}, u32[]{:S(2)}, u32[]{:S(2)}) collective-permute-start(f32[320,1024]{1,0:T(8,128)S(1)} %copy-done.49), channel_id=1, source_target_pairs={{0,8},{8,0},{1,9},{9,1},{2,10},{10,2},{3,11},{11,3},{4,12},{12,4},... | collective-permute-start | bytes 3932168 | tf_op jit(solution)/shard_map/ppermute | solution.py:240
  695.8 115.9 %collective-permute-start.12 = (f32[120,5120]{1,0:T(8,128)}, f32[120,5120]{1,0:T(8,128)}, u32[]{:S(2)}, u32[]{:S(2)}) collective-permute-start(f32[120,5120]{1,0:T(8,128)} %reduce-scatter.19.cloned.1.call-done), channel_id=1, source_target_pairs={{0,8},{8,0},{1,9},{9,1},{2,10},{10,2},{3,11},{11,3},{4,12},{12,4},... | collective-permute-start | bytes 7372808 | tf_op jit(solution)/shard_map/ppermute | solution.py:240
  696.4 107.4 %collective-permute-start.10 = (f32[120,2560]{1,0:T(8,128)}, f32[120,2560]{1,0:T(8,128)}, u32[]{:S(2)}, u32[]{:S(2)}) collective-permute-start(f32[120,2560]{1,0:T(8,128)} %reduce-scatter.21.cloned.1.call-done), channel_id=1, source_target_pairs={{0,8},{8,0},{1,9},{9,1},{2,10},{10,2},{3,11},{11,3},{4,12},{12,4},... | collective-permute-start | bytes 3686408 | tf_op jit(solution)/shard_map/ppermute | solution.py:240
  809.7 31.6 %collective-permute-start.13 = (f32[320,1024]{1,0:T(8,128)S(1)}, f32[320,1024]{1,0:T(8,128)S(1)}, u32[]{:S(2)}, u32[]{:S(2)}) collective-permute-start(f32[320,1024]{1,0:T(8,128)S(1)} %copy-done.50), channel_id=1, source_target_pairs={{0,8},{8,0},{1,9},{9,1},{2,10},{10,2},{3,11},{11,3},{4,12},{12,4},... | collective-permute-start | bytes 3932168 | tf_op jit(solution)/shard_map/ppermute | solution.py:240
  811.2 80.7 %collective-permute-start.11 = (f32[120,5120]{1,0:T(8,128)S(1)}, f32[120,5120]{1,0:T(8,128)S(1)}, u32[]{:S(2)}, u32[]{:S(2)}) collective-permute-start(f32[120,5120]{1,0:T(8,128)S(1)} %copy-done.46), channel_id=1, source_target_pairs={{0,8},{8,0},{1,9},{9,1},{2,10},{10,2},{3,11},{11,3},{4,12},{12,4},... | collective-permute-start | bytes 7372808 | tf_op jit(solution)/shard_map/ppermute | solution.py:240
  892.2 28.5 %collective-permute-start.9 = (f32[120,2688]{1,0:T(8,128)}, f32[120,2688]{1,0:T(8,128)}, u32[]{:S(2)}, u32[]{:S(2)}) collective-permute-start(f32[120,2688]{1,0:T(8,128)} %reduce-scatter.25.cloned.1.call-done), channel_id=1, source_target_pairs={{0,8},{8,0},{1,9},{9,1},{2,10},{10,2},{3,11},{11,3},{4,12},{12,4},... | collective-permute-start | bytes 3870728 | tf_op jit(solution)/shard_map/ppermute | solution.py:240
  (75 other events, 261.7 us)
Sparse Core Ops, SparseCore 0:
  15.0 39.6 all-gather.8
  57.1 56.6 all-gather.10
  116.2 37.3 all-gather.16
  155.9 35.8 all-gather.12
  194.0 56.5 all-gather.14
  252.9 37.5 all-gather.18
  323.4 57.5 reduce-scatter.14
  384.1 94.3 reduce-scatter.18
  481.5 54.8 reduce-scatter.20
  539.2 57.5 reduce-scatter.16
  599.9 94.3 reduce-scatter.22
  697.1 57.3 reduce-scatter.24

commit v2 on v1

--- a/solution.py
+++ b/solution.py
@@ -19,6 +19,7 @@
 D, HEADS, KV, HD, FF = 960, 15, 5, 64, 2560
 GROUP = HEADS // KV
 BLK = 256
+WEST = 1408
 TOKEN_SPEC = P(('dp', 'fsdp'), None, None)
 WEIGHT_SPECS = (P(None, 'fsdp'), P(None, 'fsdp', None, None), P(None, 'fsdp', None, None), P(None, 'fsdp', None, None), P(None, 'fsdp', None), P(None, 'fsdp'), P(None, 'fsdp', None), P(None, 'fsdp', None), P(None, 'fsdp', None))
 CORE_SWAP = [(i, i ^ 1) for i in range(8)]
@@ -182,6 +183,31 @@
     )(qr, kr, vb, do, cos, sin)
 
 
+def mlp_fwd_kernel(b_ref, wg_ref, wu_ref, gate_ref, up_ref, act_ref):
+    gate = dot_tn(wg_ref[...], b_ref[...])
+    up = dot_tn(wu_ref[...], b_ref[...])
+    gate_ref[...] = gate
+    up_ref[...] = up
+    act_ref[...] = (gate * jax.nn.sigmoid(gate) * up).astype(BF16)
+
+
+def mlp_forward(gate_up, b):
+    seq = b.shape[1]
+    steps = FF // 256
+    rows = pl.BlockSpec((256, seq), lambda i: (i, 0))
+    wide = jax.ShapeDtypeStruct((FF, seq), F32)
+    return pl.pallas_call(
+        mlp_fwd_kernel,
+        grid=(steps,),
+        in_specs=[pl.BlockSpec((D, seq), lambda i: (0, 0)), pl.BlockSpec((D, 256), lambda i: (0, i)), pl.BlockSpec((D, 256), lambda i: (0, steps + i))],
+        out_specs=[rows, rows, rows],
+        out_shape=[wide, wide, jax.ShapeDtypeStruct((FF, seq), BF16)],
+        compiler_params=pltpu.CompilerParams(dimension_semantics=('arbitrary',), vmem_limit_bytes=32 * 1024 * 1024),
+        cost_estimate=pl.CostEstimate(flops=10_000_000_000, bytes_accessed=38_000_000, transcendentals=5_000_000),
+        name='mlp_fwd',
+    )(b, gate_up, gate_up)
+
+
 def mlp_bwd_kernel(down_ref, grad_ref, gate_ref, up_ref, out_ref):
     dact = dot_nn(down_ref[...], grad_ref[...]).astype(BF16).astype(F32)
     gate, up = gate_ref[...], up_ref[...]
@@ -206,6 +232,65 @@
     return out.reshape(2 * FF, seq)
 
 
+def gather_kernel(shard_ref, out_ref, token_ref, send_sem, recv_sem):
+    me = lax.axis_index('fsdp')
+    over_c = me + 1 - 2 * (me % 2)
+    over_x = me + 2 - 4 * ((me // 2) % 2)
+    over_y = me + 4 - 8 * (me // 4)
+    diag = over_x + over_y - me
+    barrier = pltpu.get_barrier_semaphore()
+    for peer in (over_x, over_y, over_c):
+        pl.semaphore_signal(barrier, inc=1, device_id={'fsdp': peer}, device_id_type=pl.DeviceIdType.MESH)
+    pl.semaphore_wait(barrier, 3)
+    width = shard_ref.shape[1]
+    left, right = pl.ds(0, WEST), pl.ds(WEST, width - WEST)
+
+    def send(slot, src, dst, peer):
+        copy = pltpu.make_async_remote_copy(
+            src_ref=src, dst_ref=dst, send_sem=send_sem.at[slot], recv_sem=recv_sem.at[slot],
+            device_id={'fsdp': peer}, device_id_type=pl.DeviceIdType.MESH)
+        copy.start()
+        return copy
+
+    def relay(slot, shard, cols, peer):
+        part = out_ref.at[shard, :, cols]
+        return send(slot, part, part, peer)
+
+    own_x = send(0, shard_ref, out_ref.at[me], over_x)
+    own_y = send(1, shard_ref, out_ref.at[me], over_y)
+    own_c = send(2, shard_ref, out_ref.at[me], over_c)
+    out_ref[me] = shard_ref[...]
+    token_ref[...] = jnp.zeros_like(token_ref)
+    own_x.wait_recv()
+    diag_y = relay(3, over_x, left, over_y)
+    x_c = send(5, out_ref.at[over_x], out_ref.at[over_x], over_c)
+    own_y.wait_recv()
+    diag_x = relay(4, over_y, right, over_x)
+    y_c = send(6, out_ref.at[over_y], out_ref.at[over_y], over_c)
+    diag_y.wait_recv()
+    left_c = relay(7, diag, left, over_c)
+    diag_x.wait_recv()
+    right_c = relay(8, diag, right, over_c)
+    for copy in (own_c, x_c, y_c, left_c, right_c):
+        copy.wait_recv()
+    for copy in (own_x, own_y, own_c, diag_y, x_c, diag_x, y_c, left_c, right_c):
+        copy.wait_send()
+
+
+def gather_now(shard):
+    rows, width = shard.shape
+    out, token = pl.pallas_call(
+        gather_kernel,
+        in_specs=[pl.BlockSpec(memory_space=pltpu.VMEM)],
+        out_specs=[pl.BlockSpec(memory_space=pltpu.VMEM)] * 2,
+        out_shape=[jax.ShapeDtypeStruct((8, rows, width), shard.dtype), jax.ShapeDtypeStruct((8, 128), F32)],
+        scratch_shapes=[pltpu.SemaphoreType.DMA((9,)), pltpu.SemaphoreType.DMA((9,))],
+        compiler_params=pltpu.CompilerParams(collective_id=0, has_side_effects=True, vmem_limit_bytes=16 * 1024 * 1024),
+        name='gather_attn0',
+    )(shard)
+    return out.reshape(8 * rows, width), token
+
+
 def rms_forward(x, gain):
     inv = lax.rsqrt(jnp.mean(x * x, axis=0, keepdims=True) + NORM_EPS)
     return (x * inv * gain).astype(BF16), inv
@@ -229,16 +314,11 @@
 
 
 def row_major(a):
-    return with_layout_constraint(a, Layout(major_to_minor=(0, 1)))
+    return with_layout_constraint(a, Layout(major_to_minor=tuple(range(a.ndim))))
 
 
 def over_chips(part):
     return lax.psum_scatter(part, 'fsdp', scatter_dimension=0, tiled=True, axis_index_groups=SAME_CORE)
-
-
-def over_dp(mine):
-    peer = lax.ppermute(mine, 'dp', DP_SWAP)
-    return mine + peer
 
 
 def tie(*values):
@@ -266,9 +346,15 @@
             pieces = [w_query[l].reshape(rows, HEADS * HD), w_key[l].reshape(rows, KV * HD), w_value[l].reshape(rows, KV * HD), w_out[l]]
             if l == 0:
                 pieces.append(gains)
-            attn_w = gather(jnp.concatenate(pieces, axis=1))
+            packed = jnp.concatenate(pieces, axis=1)
+            if l:
+                attn_w = gather(packed)
+            else:
+                attn_w, token = gather_now(packed)
             gate_up = gather(jnp.concatenate([w_gate[l], w_up[l]], axis=1))
             down = gather(w_down[l])
+            if l == 0:
+                token, w_query, w_key, w_value, w_out, w_gate, w_up, w_down = tie(token, w_query, w_key, w_value, w_out, w_gate, w_up, w_down)
             weights.append((attn_w, gate_up, down))
         gain_cols = weights[0][0][:, 2560:2564].astype(F32)
         x = hidden[0].T
@@ -283,23 +369,24 @@
             x1 = (xf + dot_tn(attn_w[:, 1600:2560], o)).astype(BF16)
             x1f = x1.astype(F32)
             b, inv2 = rms_forward(x1f, g2)
-            gate = dot_tn(gate_up[:, :FF], b)
-            up = dot_tn(gate_up[:, FF:], b)
-            act = (jax.nn.silu(gate) * up).astype(BF16)
+            gate, up, act = mlp_forward(gate_up, b)
             saved.append((x, a, inv1, g1, qr, kr, vb, o, x1, b, inv2, g2, gate, up, act))
             x = (x1f + dot_tn(down, act)).astype(BF16)
         y = x
         grad = cot_out[0].T
         outs = [[None] * 3 for _ in range(layers)]
         gain_grads = [None] * (2 * layers)
-        waiting = []
+        waiting, moving = [], []
 
         def release(value):
-            if not waiting:
-                return value
             l, slot, part = waiting.pop(0)
-            value, part = tie(value, part)
-            outs[l][slot] = over_dp(part)
+            if moving:
+                done_l, done_slot, mine, peer = moving.pop(0)
+                total = (mine + peer) * grad_scale
+                value, part, outs[done_l][done_slot] = tie(value, part, total)
+            else:
+                value, part = tie(value, part)
+            moving.append((l, slot, part, lax.ppermute(part, 'dp', DP_SWAP)))
             return value
 
         for l in reversed(range(layers)):
@@ -309,11 +396,20 @@
             other_down = row_major(dot_nt(core_half(act, 1 - core), wide))
             grad, other_down = tie(grad, other_down)
             sent_down = to_peer(other_down)
-            dgu = mlp_backward(down, grad, gate, up)
-            act_mine, dgu = tie(core_half(act, core), dgu)
-            mine_down = row_major(dot_nt(act_mine, wide) + sent_down)
+            act_mine = core_half(act, core)
+            if l == 0:
+                dgu = mlp_backward(down, grad, gate, up)
+                act_mine, dgu = tie(act_mine, dgu)
+                mine_down = row_major(dot_nt(act_mine, wide) + sent_down)
+            else:
+                mine_down = row_major(dot_nt(act_mine, wide) + sent_down)
+                grad, mine_down = tie(grad, mine_down)
+                dgu = mlp_backward(down, grad, gate, up)
             other_gu = row_major(dot_nt(core_half(b, 1 - core), dgu))
-            dgu, mine_down, other_gu = tie(dgu, mine_down, other_gu)
+            if l == 0:
+                dgu, mine_down, other_gu = tie(dgu, mine_down, other_gu)
+            else:
+                dgu, other_gu = tie(dgu, other_gu)
             waiting.append((l, 2, over_chips(mine_down)))
             sent_gu = to_peer(other_gu)
             db = dot_nn(gate_up, dgu).astype(BF16).astype(F32)
@@ -339,7 +435,8 @@
             dxn, gain_grads[2 * l] = rms_backward(x.astype(F32), inv1, g1, da)
             grad = (dmid.astype(F32) + dxn).astype(BF16)
             a_mine, grad = tie(core_half(a, core), grad)
-            parts = [dot_nt(a_mine, dqkv) + sent_qkv, mine_o]
+            mine_qkv = dot_nt(a_mine, dqkv) + sent_qkv
+            parts = [mine_qkv, mine_o]
             if l == 0:
                 cols = jnp.pad(jnp.stack(gain_grads, axis=1), ((0, 0), (0, 124)))
                 parts.append(core_half(cols, core) + to_peer(core_half(cols, 1 - core)))
@@ -348,11 +445,13 @@
             if l == 0:
                 part = release(release(part))
             waiting.append((l, 0, over_chips(part)))
-        for l, slot, part in waiting:
-            outs[l][slot] = over_dp(part)
-        ra = [o[0] * grad_scale for o in outs]
-        rg = [o[1] * grad_scale for o in outs]
-        rd = [o[2][:, :D] * grad_scale for o in outs]
+        (l, slot, part), = waiting
+        moving.append((l, slot, part, lax.ppermute(part, 'dp', DP_SWAP)))
+        for l, slot, mine, peer in moving:
+            outs[l][slot] = (mine + peer) * grad_scale
+        ra = [o[0] for o in outs]
+        rg = [o[1] for o in outs]
+        rd = [o[2][:, :D] for o in outs]
         gain = ra[0][:, 2560:2564]
         stack = lambda parts: jnp.stack(parts)
         return (

time: 947 us -> 774 us (0.82)
  waiting for transfers between devices: 387 us -> 175 us
  Pallas kernels: 177 us -> 256 us
  matrix products: 235 us -> 187 us
    optimization_barrier x3, waiting for transfers between devices: 92.9 us -> 4.11 us  [tie(): return lax.optimization_barrier(values)]
    pallas_call x0 -> x3, Pallas kernels: none -> 78.9 us  [the longest x1 47.7 us: gather_now(): pl.pallas_call(gather_kernel, in_specs=[pl.BlockSpec(memory_space=pltpu.V...]
    all_gather x6 -> x5, waiting for transfers between devices: 105 us -> 26.5 us  [gather(): return lax.all_gather(shard, 'fsdp', axis=0, tiled=True)]
    ppermute x6, waiting for transfers between devices: 188 us -> 131 us  [the longest x5 106 us: release(): moving.append((l, slot, part, lax.ppermute(part, 'dp', DP_SWAP)))]
    dot_general x10 -> x6, matrix products: 94 us -> 49.3 us  [dot_tn(): lax.dot_general(a, b, (((0,), (0,)), ((), ())), preferred_element_type=F32)]
    unnamed x200 -> x199, local copies, waits for them, and re-layouts: 22.1 us -> 32.1 us
  transfers between devices with their start and end apart: 27 -> 26, of which waited for: 12 -> 11; matrix products, arithmetic and copies ran while one was open for 33% -> 34% of each run, Pallas kernels for 19% -> 32%
where the time goes in v2:
time: 774 us; the launch traced here: 764 us
  Pallas kernels  256 us (33%)
  matrix products  187 us (24%)
  waiting for transfers between devices  175 us (23%)
  local copies, waits for them, and re-layouts  74.5 us (10%)
  other arithmetic  45.5 us (6%)
  between operations  15.6 us (2%)
  starting transfers between devices  11 us (1%)
    ppermute x5, waiting for transfers between devices, release(): moving.append((l, slot, part, lax.ppermute(part, 'dp', DP_SWAP)))  106 us
    pallas_call x2, Pallas kernels, attention_backward(): pl.pallas_call(attn_bwd_kernel, grid=(KV,), in_specs=[head_spec(seq, 0, G...  89.8 us
    dot_general x16, matrix products, dot_nt(): lax.dot_general(a, b, (((1,), (1,)), ((), ())), preferred_element_type=F32)  81.7 us
    pallas_call x2, Pallas kernels, attention_forward(): pl.pallas_call(attn_fwd_kernel, grid=(KV,), in_specs=[head_spec(seq, 0, G...  58.2 us
    dot_general x6, matrix products, dot_nn(): lax.dot_general(a, b, (((1,), (0,)), ((), ())), preferred_element_type=F32)  56.1 us
    dot_general x6, matrix products, dot_tn(): lax.dot_general(a, b, (((0,), (0,)), ((), ())), preferred_element_type=F32)  49.3 us
    pallas_call x1, Pallas kernels, gather_now(): pl.pallas_call(gather_kernel, in_specs=[pl.BlockSpec(memory_space=pltpu.V...  47.7 us
    unnamed x199, local copies, waits for them, and re-layouts  32.1 us
  transfers between devices with their start and end apart: 26, of which 11 were waited for; matrix products, arithmetic and copies ran while one was open for 34% of the time, Pallas kernels for 32%

profile of v2, /device:TPU:0, one launch (start us, length us, event | category | flops | bytes accessed | tf_op | source)
XLA Modules:
  0.0 764.0 jit_solution(14989907334954777708)
XLA Ops:
  19.0 47.7 %gather_attn0.1 = (bf16[8,120,2688]{2,1,0:T(8,128)(2,1)S(1)}, f32[8,128]{1,0:T(8,128)}) custom-call(bf16[120,2688]{1,0:T(8,128)(2,1)S(1)} %concatenate.24.shard_ref), custom_call_target="tpu_custom_call" | custom-call | tf_op jit(solution)/shard_map/gather_attn0/pallas_call | solution.py:282
  71.6 5.6 fusion.52.q_ref.k_ref.v_ref
  77.8 29.0 %attn_fwd.2 = (bf16[960,1024]{1,0:T(8,128)(2,1)S(1)}, bf16[320,1024]{1,0:T(8,128)(2,1)S(1)}, bf16[320,1024]{1,0:T(8,128)(2,1)S(1)}, bf16[960,1024]{1,0:T(8,128)(2,1)S(1)}) custom-call(f32[1600,1024]{1,0:T(8,128)} %fusion.52.q_ref.k_ref.v_ref, f32[1600,1024]{1,0:T(8,128)} %fusion.52.q_ref.k_ref.v_ref, f32[1600,1024]{1,0:T(8,128)} %fusion.52.q_ref.k_ref.v_ref, ...), custom_call_target="tpu_custom_call" | custom-call | flops 20000000000 | bytes 14000000 | tf_op jit(solution)/shard_map/attn_fwd/pallas_call | solution.py:156
  106.8 5.3 fusion.39
  114.9 4.6 copy-done.13
  119.5 15.4 %mlp_fwd.2 = (f32[2560,1024]{1,0:T(8,128)}, f32[2560,1024]{1,0:T(8,128)}, bf16[2560,1024]{1,0:T(8,128)(2,1)S(1)}) custom-call(bf16[960,1024]{1,0:T(8,128)(2,1)S(1)} %fusion.14.b_ref, bf16[960,5120]{1,0:T(8,128)(2,1)S(1)} %copy-done.13, bf16[960,5120]{1,0:T(8,128)(2,1)S(1)} %copy-done.13), custom_call_target="tpu_custom_call" | custom-call | flops 10000000000 | bytes 38000000 | tf_op jit(solution)/shard_map/mlp_fwd/pallas_call | solution.py:199
  137.2 10.7 %fusion.42 = (f32[1024]{0:T(1024)S(1)}, bf16[960,1024]{1,0:T(8,128)(2,1)S(1)}, f32[1024,960]{0,1:T(8,128)}) fusion(bf16[960,1024]{1,0:T(8,128)(2,1)} %get-tuple-element.212, bf16[2560,1024]{1,0:T(8,128)(2,1)} %copy-done.8, bf16[1,2560,960]{2,1,0:T(8,128)(2,1)} %all-gather.14.cloned.1.call-done), kind=kOutput, calls=%fused_computation.71 | convolution fusion | flops 5039062016 | bytes 18026496 | tf_op jit(solution)/shard_map/dot_general | solution.py:52
  149.7 14.4 %all-gather.10.cloned.1.call-done = bf16[960,2560]{1,0:T(8,128)(2,1)} async-done(((bf16[120,2560]{1,0:T(8,128)(2,1)}), bf16[960,2560]{1,0:T(8,128)(2,1)}) %all-gather.10.cloned.1.call-update) | async-done | bytes 4915216 | tf_op jit(solution)/shard_map/all_gather | solution.py:329
  164.1 7.5 fusion.48.q_ref.k_ref.v_ref
  171.6 29.1 %attn_fwd.3 = (bf16[960,1024]{1,0:T(8,128)(2,1)S(1)}, bf16[320,1024]{1,0:T(8,128)(2,1)S(1)}, bf16[320,1024]{1,0:T(8,128)(2,1)S(1)}, bf16[960,1024]{1,0:T(8,128)(2,1)S(1)}) custom-call(f32[1600,1024]{1,0:T(8,128)} %fusion.48.q_ref.k_ref.v_ref, f32[1600,1024]{1,0:T(8,128)} %fusion.48.q_ref.k_ref.v_ref, f32[1600,1024]{1,0:T(8,128)} %fusion.48.q_ref.k_ref.v_ref, ...), custom_call_target="tpu_custom_call" | custom-call | flops 20000000000 | bytes 14000000 | tf_op jit(solution)/shard_map/attn_fwd/pallas_call | solution.py:156
  200.8 7.8 %fusion.37 = (f32[1024]{0:T(1024)S(1)}, bf16[960,1024]{1,0:T(8,128)(2,1)S(1)}, f32[960,1024]{1,0:T(8,128)}) fusion(bf16[960,1024]{1,0:T(8,128)(2,1)S(1)} %copy-done.31, bf16[960,1024]{1,0:T(8,128)(2,1)S(1)} %get-tuple-element.101, bf16[960,2560]{1,0:T(8,128)(2,1)} %all-gather.10.cloned.1.call-done), kind=kOutput, calls=%fused_computation.66 | convolution fusion | flops 1893334016 | bytes 11800576 | tf_op jit(solution)/shard_map/dot_general | solution.py:52
  210.3 12.1 %all-gather.12.cloned.1.call-done.wg_ref.wu_ref = bf16[960,5120]{1,0:T(8,128)(2,1)} async-done(((bf16[120,5120]{1,0:T(8,128)(2,1)}), bf16[960,5120]{1,0:T(8,128)(2,1)}) %all-gather.12.cloned.1.call-update) | async-done | bytes 9830416 | tf_op jit(solution)/shard_map/all_gather | solution.py:329
  222.4 3.8 copy-done.14
  226.2 15.8 %mlp_fwd.3 = (f32[2560,1024]{1,0:T(8,128)}, f32[2560,1024]{1,0:T(8,128)}, bf16[2560,1024]{1,0:T(8,128)(2,1)S(1)}) custom-call(bf16[960,1024]{1,0:T(8,128)(2,1)S(1)} %fusion.15.b_ref, bf16[960,5120]{1,0:T(8,128)(2,1)S(1)} %copy-done.14, bf16[960,5120]{1,0:T(8,128)(2,1)S(1)} %copy-done.14), custom_call_target="tpu_custom_call" | custom-call | flops 10000000000 | bytes 38000000 | tf_op jit(solution)/shard_map/mlp_fwd/pallas_call | solution.py:199
  249.9 8.3 %collective-permute-done = f32[1280,1024]{1,0:T(8,128)S(1)} collective-permute-done((f32[1280,1024]{1,0:T(8,128)S(1)}, f32[1280,1024]{1,0:T(8,128)S(1)}, u32[]{:S(2)}, u32[]{:S(2)}) %collective-permute-start) | collective-permute-done | bytes 5242912 | tf_op jit(solution)/shard_map/ppermute | solution.py:313
  258.2 4.8 convolution_add_fusion.3
  265.4 14.3 %mlp_bwd.2 = bf16[2,2560,1024]{2,1,0:T(8,128)(2,1)S(1)} custom-call(bf16[2560,960]{1,0:T(8,128)(2,1)S(1)} %bitcast.220, bf16[960,1024]{1,0:T(8,128)(2,1)S(1)} %bitcast.218, f32[2560,1024]{1,0:T(8,128)} %get-tuple-element.109.gate_ref, f32[2560,1024]{1,0:T(8,128)} %get-tuple-element.110.up_ref), custom_call_target="tpu_custom_call" | custom-call | flops 5000000000 | bytes 38000000 | tf_op jit(solution)/shard_map/mlp_bwd/pallas_call | solution.py:222
  279.7 7.8 %fusion.96 = f32[480,5120]{1,0:T(8,128)} fusion(bf16[480,1024]{1,0:T(8,128)(2,1)S(1)} %bitcast.256, bf16[5120,1024]{1,0:T(8,128)(2,1)S(1)} %bitcast.209), kind=kOutput, calls=%fused_computation.201 | convolution fusion | flops 5033164800 | bytes 21299200 | tf_op jit(solution)/shard_map/dot_general | solution.py:48
  290.5 18.3 %fusion.29 = (f32[960]{0:T(1024)}, f32[1024]{0:T(1024)S(1)}, bf16[960,1024]{1,0:T(8,128)(2,1)S(1)}) fusion(bf16[960,1024]{1,0:T(8,128)(2,1)S(1)} %copy-done.34, f32[1024]{0:T(1024)S(1)} %add_rsqrt_fusion, f32[960]{0:T(1024)S(1)} %bitcast.278, bf16[960,5120]{1,0:T(8,128)(2,1)} %all-gather.12.cloned.1.call-done.wg_ref.wu_ref, bf16[5120,1024]{1,0:T(8,128)(2,1)} %bitcast.210), kind=kOutput, calls=%fused_computation.58 | convolution fusion | flops 10075174912 | bytes 24264192 | tf_op jit(solution)/shard_map/dot_general | solution.py:44
  312.6 10.2 %convolution_add_fusion.1 = f32[480,5120]{1,0:T(8,128)} fusion(f32[480,5120]{1,0:T(8,128)} %collective-permute-done.1, bf16[480,1024]{1,0:T(8,128)(2,1)S(1)} %bitcast.252, bf16[5120,1024]{1,0:T(8,128)(2,1)S(1)} %bitcast.213), kind=kOutput, calls=%fused_computation.11 | convolution fusion | flops 5035622400 | bytes 31129600 | tf_op jit(solution)/shard_map/dot_general | solution.py:48
  326.3 5.5 convolution_convert_fusion.3.do_ref
  331.8 44.7 %attn_bwd.2 = (bf16[960,1024]{1,0:T(8,128)(2,1)S(1)}, bf16[320,1024]{1,0:T(8,128)(2,1)S(1)}, bf16[320,1024]{1,0:T(8,128)(2,1)S(1)}) custom-call(bf16[960,1024]{1,0:T(8,128)(2,1)} %copy-done.16, bf16[320,1024]{1,0:T(8,128)(2,1)S(1)} %copy-done.18, bf16[320,1024]{1,0:T(8,128)(2,1)S(1)} %copy-done.20, bf16[960,1024]{1,0:T(8,128)(2,1)} %convolution_convert_fusion.3.do_ref, ...), custom_call_target="tpu_custom_call" | custom-call | flops 40000000000 | bytes 14000000 | tf_op jit(solution)/shard_map/attn_bwd/pallas_call | solution.py:173
  386.2 4.9 fusion.30
  394.3 3.2 pad_maximum_fusion
  397.6 3.2 constant_dynamic-slice_fusion.7
  400.8 5.1 fusion.56
  407.7 14.6 %mlp_bwd.3 = bf16[2,2560,1024]{2,1,0:T(8,128)(2,1)S(1)} custom-call(bf16[2560,960]{1,0:T(8,128)(2,1)S(1)} %bitcast.223, bf16[960,1024]{1,0:T(8,128)(2,1)S(1)} %fusion.25.grad_ref, f32[2560,1024]{1,0:T(8,128)} %get-tuple-element.134.gate_ref, f32[2560,1024]{1,0:T(8,128)} %get-tuple-element.135.up_ref), custom_call_target="tpu_custom_call" | custom-call | flops 5000000000 | bytes 38000000 | tf_op jit(solution)/shard_map/mlp_bwd/pallas_call | solution.py:222
  422.3 7.8 %fusion.100 = f32[480,5120]{1,0:T(8,128)} fusion(bf16[480,1024]{1,0:T(8,128)(2,1)S(1)} %bitcast.258, bf16[5120,1024]{1,0:T(8,128)(2,1)S(1)} %bitcast.206), kind=kOutput, calls=%fused_computation.205 | convolution fusion | flops 5033164800 | bytes 21299200 | tf_op jit(solution)/shard_map/dot_general | solution.py:48
  430.1 4.8 convolution_add_fusion.2
  439.5 26.9 %collective-permute-done.5 = f32[320,1024]{1,0:T(8,128)S(1)} collective-permute-done((f32[320,1024]{1,0:T(8,128)}, f32[320,1024]{1,0:T(8,128)S(1)}, u32[]{:S(2)}, u32[]{:S(2)}) %collective-permute-start.5) | collective-permute-done | bytes 1310752 | tf_op jit(solution)/shard_map/ppermute | solution.py:389
  467.7 16.8 %fusion.31 = (f32[960]{0:T(1024)S(1)}, f32[1024]{0:T(1024)S(1)}, bf16[960,1024]{1,0:T(8,128)(2,1)S(1)}) fusion(bf16[960,1024]{1,0:T(8,128)(2,1)S(1)} %copy-done.29, f32[1024]{0:T(1024)S(1)} %copy-done.72, f32[960]{0:T(1024)S(1)} %bitcast.272, bf16[960,5120]{1,0:T(8,128)(2,1)} %all-gather.8.cloned.1.call-done.wg_ref.wu_ref, bf16[5120,1024]{1,0:T(8,128)(2,1)} %bitcast.207), kind=kOutput, calls=%fused_computation.60 | convolution fusion | flops 10075174912 | bytes 24264192 | tf_op jit(solution)/shard_map/dot_general | solution.py:44
  486.9 4.4 fusion.101
  491.4 13.6 %convolution_add_fusion = f32[480,5120]{1,0:T(8,128)} fusion(f32[480,5120]{1,0:T(8,128)} %collective-permute-done.6, bf16[480,1024]{1,0:T(8,128)(2,1)S(1)} %bitcast.249, bf16[5120,1024]{1,0:T(8,128)(2,1)} %bitcast.208), kind=kOutput, calls=%fused_computation.10 | convolution fusion | flops 5035622400 | bytes 31129600 | tf_op jit(solution)/shard_map/dot_general | solution.py:48
  509.5 5.2 convolution_convert_fusion.2.do_ref
  514.7 45.0 %attn_bwd.3 = (bf16[960,1024]{1,0:T(8,128)(2,1)S(1)}, bf16[320,1024]{1,0:T(8,128)(2,1)S(1)}, bf16[320,1024]{1,0:T(8,128)(2,1)S(1)}) custom-call(bf16[960,1024]{1,0:T(8,128)(2,1)} %copy-done.15, bf16[320,1024]{1,0:T(8,128)(2,1)S(1)} %get-tuple-element.148.k_ref, bf16[320,1024]{1,0:T(8,128)(2,1)S(1)} %get-tuple-element.149.v_ref, ...), custom_call_target="tpu_custom_call" | custom-call | flops 40000000000 | bytes 14000000 | tf_op jit(solution)/shard_map/attn_bwd/pallas_call | solution.py:173
  566.3 3.3 add.220
  569.6 3.7 fusion.103
  574.9 5.4 fusion.32
  584.9 4.2 fusion.19
  589.1 14.0 %collective-permute-done.11 = f32[120,2560]{1,0:T(8,128)} collective-permute-done((f32[120,2560]{1,0:T(8,128)}, f32[120,2560]{1,0:T(8,128)}, u32[]{:S(2)}, u32[]{:S(2)}) %collective-permute-start.11) | collective-permute-done | bytes 1228832 | tf_op jit(solution)/shard_map/ppermute | solution.py:389
  608.6 6.1 convolution_add_fusion.4
  614.7 6.7 concatenate.31
  622.9 28.9 %collective-permute-done.12 = f32[320,1024]{1,0:T(8,128)S(1)} collective-permute-done((f32[320,1024]{1,0:T(8,128)}, f32[320,1024]{1,0:T(8,128)S(1)}, u32[]{:S(2)}, u32[]{:S(2)}) %collective-permute-start.12) | collective-permute-done | bytes 1310752 | tf_op jit(solution)/shard_map/ppermute | solution.py:389
  654.5 4.1 reduce-scatter.23.cloned.1.call-done
  660.1 12.4 %fusion.54 = bf16[1,1024,960]{1,2,0:T(8,128)(2,1)} fusion(f32[960,1024]{1,0:T(8,128)} %get-tuple-element.259, f32[1024,960]{0,1:T(8,128)} %get-tuple-element.258, f32[960,1024]{1,0:T(8,128)} %get-tuple-element.257, bf16[1,1024,960]{1,2,0:T(8,128)(2,1)S(1)} %copy-done.23, bf16[2560,1024]{1,0:T(8,128)(2,1)} %copy-done.7, ...), kind=kOutput, calls=%fused_computation.95 | convolution fusion | flops 5044961280 | bytes 25886720 | tf_op jit(solution)/shard_map/dot_general | solution.py:52
  679.5 34.4 %collective-permute-done.14 = f32[120,5120]{1,0:T(8,128)S(1)} collective-permute-done((f32[120,5120]{1,0:T(8,128)}, f32[120,5120]{1,0:T(8,128)S(1)}, u32[]{:S(2)}, u32[]{:S(2)}) %collective-permute-start.14) | collective-permute-done | bytes 2457632 | tf_op jit(solution)/shard_map/ppermute | solution.py:389
  714.1 4.9 reduce-scatter.25.cloned.1.call-done
  724.4 24.8 %collective-permute-done.13 = f32[120,2688]{1,0:T(8,128)} collective-permute-done((f32[120,2688]{1,0:T(8,128)}, f32[120,2688]{1,0:T(8,128)}, u32[]{:S(2)}, u32[]{:S(2)}) %collective-permute-start.13) | collective-permute-done | bytes 1290272 | tf_op jit(solution)/shard_map/ppermute | solution.py:449
  (353 shorter events, 117.2 us)
Async XLA Ops:
  7.2 107.7 %all-gather.8.cloned.1.call-start = ((), (), s32[]{:S(2)}) async-start(), calls=%async_computation.6 | async-start | bytes 11059200 | tf_op jit(solution)/shard_map/all_gather | solution.py:329
  9.9 127.4 %all-gather.14.cloned.1.call-start = ((), (), s32[]{:S(2)}) async-start(), calls=%async_computation.11 | async-start | bytes 5898240 | tf_op jit(solution)/shard_map/all_gather | solution.py:329
  10.8 153.3 %all-gather.10.cloned.1.call-start = ((), (), s32[]{:S(2)}) async-start(), calls=%async_computation.7 | async-start | bytes 5529600 | tf_op jit(solution)/shard_map/all_gather | solution.py:329
  13.6 208.8 %all-gather.12.cloned.1.call-start = ((), (), s32[]{:S(2)}) async-start(), calls=%async_computation.8 | async-start | bytes 11059200 | tf_op jit(solution)/shard_map/all_gather | solution.py:329
  15.1 54.1 %copy-start.21 = (bf16[1,1024,960]{1,2,0:T(8,128)(2,1)S(1)}, bf16[1,1024,960]{1,2,0:T(8,128)(2,1)}, u32[]{:S(2)}) copy-start(bf16[1,1024,960]{1,2,0:T(8,128)(2,1)} %param.11) | copy-start | bytes 5898244
  15.1 247.8 %all-gather.16.cloned.1.call-start = ((), (), s32[]{:S(2)}) async-start(), calls=%async_computation.12 | async-start | bytes 5898240 | tf_op jit(solution)/shard_map/all_gather | solution.py:329
  17.3 361.5 %reduce-scatter.15.cloned.1.call-start = ((), (), s32[]{:S(2)}) async-start(), calls=%async_computation.9 | async-start | bytes 6553600 | tf_op jit(solution)/shard_map/reduce_scatter | solution.py:321
  69.2 43.7 %copy-start.77 = (f32[960,1]{0,1:T(1,128)}, f32[960,1]{0,1:T(1,128)S(1)}, u32[]{:S(2)}) copy-start(f32[960,1]{0,1:T(1,128)S(1)} %get-tuple-element.249) | copy-start | bytes 11524
  69.2 78.8 %copy-start.79 = (f32[960,1]{0,1:T(1,128)}, f32[960,1]{0,1:T(1,128)S(1)}, u32[]{:S(2)}) copy-start(f32[960,1]{0,1:T(1,128)S(1)} %get-tuple-element.248) | copy-start | bytes 11524
  77.8 29.1 %copy-start.22 = (bf16[1,1024,960]{1,2,0:T(8,128)(2,1)S(1)}, bf16[1,1024,960]{1,2,0:T(8,128)(2,1)}, u32[]{:S(2)}) copy-start(bf16[1,1024,960]{1,2,0:T(8,128)(2,1)} %param.11) | copy-start | bytes 5898244
  112.8 22.1 %copy-start.71 = (f32[1024]{0:T(1024)}, f32[1024]{0:T(1024)S(1)}, u32[]{:S(2)}) copy-start(f32[1024]{0:T(1024)S(1)} %add_rsqrt_fusion.2) | copy-start | bytes 12292
  114.8 20.1 %copy-start.2 = (bf16[960,1024]{1,0:T(8,128)(2,1)}, bf16[960,1024]{1,0:T(8,128)(2,1)S(1)}, u32[]{:S(2)}) copy-start(bf16[960,1024]{1,0:T(8,128)(2,1)S(1)} %fusion.14.b_ref) | copy-start | bytes 5898244
  148.0 23.6 %copy-start.83 = (f32[1024]{0:T(1024)}, f32[1024]{0:T(1024)S(1)}, u32[]{:S(2)}) copy-start(f32[1024]{0:T(1024)S(1)} %get-tuple-element.209) | copy-start | bytes 12292
  149.7 21.8 %copy-start.27 = (bf16[960,1024]{1,0:T(8,128)(2,1)}, bf16[960,1024]{1,0:T(8,128)(2,1)S(1)}, u32[]{:S(2)}) copy-start(bf16[960,1024]{1,0:T(8,128)(2,1)S(1)} %fusion.13) | copy-start | bytes 5898244
  171.6 29.2 %copy-start.31 = (bf16[960,1024]{1,0:T(8,128)(2,1)S(1)}, bf16[960,1024]{1,0:T(8,128)(2,1)}, u32[]{:S(2)}) copy-start(bf16[960,1024]{1,0:T(8,128)(2,1)} %copy-done.30) | copy-start | bytes 5898244
  248.2 10.0 %collective-permute-start = (f32[1280,1024]{1,0:T(8,128)S(1)}, f32[1280,1024]{1,0:T(8,128)S(1)}, u32[]{:S(2)}, u32[]{:S(2)}) collective-permute-start(f32[1280,1024]{1,0:T(8,128)S(1)} %fusion.59), channel_id=1, source_target_pairs={{0,1},{1,0},{2,3},{3,2},{4,5},{5,4},{6,7},{7,6},{8,9},{9,8},{10,11... | collective-permute-start | bytes 15728648 | tf_op jit(solution)/shard_map/ppermute | solution.py:313
  265.4 14.3 %copy-start.65 = (bf16[4,1,120,1024]{3,2,1,0:T(8,128)(2,1)S(1)}, bf16[4,1,120,1024]{3,2,1,0:T(8,128)(2,1)}, u32[]{:S(2)}) copy-start(bf16[4,1,120,1024]{3,2,1,0:T(8,128)(2,1)} %get-tuple-element.231) | copy-start | bytes 2949124
  287.5 25.0 %collective-permute-start.1 = (f32[480,5120]{1,0:T(8,128)}, f32[480,5120]{1,0:T(8,128)}, u32[]{:S(2)}, u32[]{:S(2)}) collective-permute-start(f32[480,5120]{1,0:T(8,128)} %fusion.96), channel_id=1, source_target_pairs={{0,1},{1,0},{2,3},{3,2},{4,5},{5,4},{6,7},{7,6},{8,9},{9,8},{10,11... | collective-permute-start | bytes 29491208 | tf_op jit(solution)/shard_map/ppermute | solution.py:313
  287.7 199.3 %reduce-scatter.19.cloned.1.call-start = ((), (), s32[]{:S(2)}) async-start(), calls=%async_computation.13 | async-start | bytes 12288000
  287.7 24.8 %slice-start = ((s8[10485760]{0:T(1024)(128)(4,1)}), s8[4194304]{0:T(1024)(128)(4,1)S(1)}, s32[]{:S(2)}) async-start(s8[10485760]{0:T(1024)(128)(4,1)} %bitcast.211), calls=%async_computation.17 | async-start | bytes 8388608
  290.5 22.0 %slice-start.1 = ((s8[10485760]{0:T(1024)(128)(4,1)}), s8[4194304]{0:T(1024)(128)(4,1)S(1)}, s32[]{:S(2)}) async-start(s8[10485760]{0:T(1024)(128)(4,1)} %bitcast.211), calls=%async_computation.18 | async-start | bytes 8388608
  290.5 22.0 %slice-start.2 = ((s8[10485760]{0:T(1024)(128)(4,1)}), s8[2097152]{0:T(1024)(128)(4,1)S(1)}, s32[]{:S(2)}) async-start(s8[10485760]{0:T(1024)(128)(4,1)} %bitcast.211), calls=%async_computation.19 | async-start | bytes 4194304
  322.8 242.2 %reduce-scatter.21.cloned.1.call-start = ((), (), s32[]{:S(2)}) async-start(), calls=%async_computation.14 | async-start | bytes 6144000
  326.0 58.0 %collective-permute-start.2 = (f32[480,960]{1,0:T(8,128)}, f32[480,960]{1,0:T(8,128)}, u32[]{:S(2)}, u32[]{:S(2)}) collective-permute-start(f32[480,960]{1,0:T(8,128)} %fusion.97), channel_id=1, source_target_pairs={{0,1},{1,0},{2,3},{3,2},{4,5},{5,4},{6,7},{7,6},{8,9},{9,8},{10,11... | collective-permute-start | bytes 5529608 | tf_op jit(solution)/shard_map/ppermute | solution.py:313
  386.1 6.2 collective-permute-start.3
  397.6 223.9 %reduce-scatter.17.cloned.1.call-start = ((), (), s32[]{:S(2)}) async-start(), calls=%async_computation.10 | async-start | bytes 6553600 | tf_op jit(solution)/shard_map/reduce_scatter | solution.py:321
  406.0 24.1 %collective-permute-start.4 = (f32[1280,1024]{1,0:T(8,128)}, f32[1280,1024]{1,0:T(8,128)S(1)}, u32[]{:S(2)}, u32[]{:S(2)}) collective-permute-start(f32[1280,1024]{1,0:T(8,128)} %fusion.56), channel_id=1, source_target_pairs={{0,1},{1,0},{2,3},{3,2},{4,5},{5,4},{6,7},{7,6},{8,9},{9,8},{10,11... | collective-permute-start | bytes 15728648 | tf_op jit(solution)/shard_map/ppermute | solution.py:313
  434.8 56.6 %collective-permute-start.6 = (f32[480,5120]{1,0:T(8,128)}, f32[480,5120]{1,0:T(8,128)}, u32[]{:S(2)}, u32[]{:S(2)}) collective-permute-start(f32[480,5120]{1,0:T(8,128)} %fusion.100), channel_id=1, source_target_pairs={{0,1},{1,0},{2,3},{3,2},{4,5},{5,4},{6,7},{7,6},{8,9},{9,8},{10,11... | collective-permute-start | bytes 29491208 | tf_op jit(solution)/shard_map/ppermute | solution.py:313
  434.8 223.8 %reduce-scatter.23.cloned.1.call-start = ((), (), s32[]{:S(2)}) async-start(), calls=%async_computation.15 | async-start | bytes 12288000
  434.9 31.4 %copy-start.54 = (f32[320,1024]{1,0:T(8,128)S(1)}, f32[320,1024]{1,0:T(8,128)}, u32[]{:S(2)}) copy-start(f32[320,1024]{1,0:T(8,128)} %reduce-scatter.15.cloned.1.call-done) | copy-start | bytes 3932164
  434.9 31.4 %collective-permute-start.5 = (f32[320,1024]{1,0:T(8,128)}, f32[320,1024]{1,0:T(8,128)S(1)}, u32[]{:S(2)}, u32[]{:S(2)}) collective-permute-start(f32[320,1024]{1,0:T(8,128)} %reduce-scatter.15.cloned.1.call-done), channel_id=1, source_target_pairs={{0,8},{8,0},{1,9},{9,1},{2,10},{10,2},{3,11},{11,3},{4,12},{12,4},... | collective-permute-start | bytes 3932168 | tf_op jit(solution)/shard_map/ppermute | solution.py:389
  436.4 31.3 %copy-start.29 = (bf16[960,1024]{1,0:T(8,128)(2,1)S(1)}, bf16[960,1024]{1,0:T(8,128)(2,1)}, u32[]{:S(2)}) copy-start(bf16[960,1024]{1,0:T(8,128)(2,1)} %get-tuple-element.212) | copy-start | bytes 5898244
  436.4 31.3 %copy-start.72 = (f32[1024]{0:T(1024)S(1)}, f32[1024]{0:T(1024)}, u32[]{:S(2)}) copy-start(f32[1024]{0:T(1024)} %copy-done.71) | copy-start | bytes 12292
  436.4 31.3 %copy-start.78 = (f32[960,1]{0,1:T(1,128)S(1)}, f32[960,1]{0,1:T(1,128)}, u32[]{:S(2)}) copy-start(f32[960,1]{0,1:T(1,128)} %copy-done.77) | copy-start | bytes 11524
  467.7 16.8 %copy-start.82 = (f32[1024]{0:T(1024)S(1)}, f32[1024]{0:T(1024)}, u32[]{:S(2)}) copy-start(f32[1024]{0:T(1024)} %copy-done.81) | copy-start | bytes 12292
  505.0 213.9 %reduce-scatter.25.cloned.1.call-start = ((), (), s32[]{:S(2)}) async-start(), calls=%async_computation.16 | async-start | bytes 6451200
  508.0 55.2 %collective-permute-start.7 = (f32[120,5120]{1,0:T(8,128)}, f32[120,5120]{1,0:T(8,128)S(1)}, u32[]{:S(2)}, u32[]{:S(2)}) collective-permute-start(f32[120,5120]{1,0:T(8,128)} %reduce-scatter.19.cloned.1.call-done), channel_id=1, source_target_pairs={{0,8},{8,0},{1,9},{9,1},{2,10},{10,2},{3,11},{11,3},{4,12},{12,4},... | collective-permute-start | bytes 7372808 | tf_op jit(solution)/shard_map/ppermute | solution.py:389
  509.5 56.8 %collective-permute-start.8 = (f32[480,960]{1,0:T(8,128)}, f32[480,960]{1,0:T(8,128)}, u32[]{:S(2)}, u32[]{:S(2)}) collective-permute-start(f32[480,960]{1,0:T(8,128)} %fusion.101), channel_id=1, source_target_pairs={{0,1},{1,0},{2,3},{3,2},{4,5},{5,4},{6,7},{7,6},{8,9},{9,8},{10,11... | collective-permute-start | bytes 5529608 | tf_op jit(solution)/shard_map/ppermute | solution.py:313
  573.4 9.7 %copy-start.85 = (f32[960]{0:T(1024)S(1)}, f32[960]{0:T(1024)}, u32[]{:S(2)}) copy-start(f32[960]{0:T(1024)} %get-tuple-element.205) | copy-start | bytes 11524
  573.4 9.7 %copy-start.86 = (f32[960]{0:T(1024)S(1)}, f32[960]{0:T(1024)}, u32[]{:S(2)}) copy-start(f32[960]{0:T(1024)} %get-tuple-element.203) | copy-start | bytes 11524
  573.4 34.5 %collective-permute-start.9 = (f32[480,1600]{1,0:T(8,128)}, f32[480,1600]{1,0:T(8,128)}, u32[]{:S(2)}, u32[]{:S(2)}) collective-permute-start(f32[480,1600]{1,0:T(8,128)} %fusion.103), channel_id=1, source_target_pairs={{0,1},{1,0},{2,3},{3,2},{4,5},{5,4},{6,7},{7,6},{8,9},{9,8},{10,11... | collective-permute-start | bytes 9216008 | tf_op jit(solution)/shard_map/ppermute | solution.py:313
  573.4 29.7 %collective-permute-start.11 = (f32[120,2560]{1,0:T(8,128)}, f32[120,2560]{1,0:T(8,128)}, u32[]{:S(2)}, u32[]{:S(2)}) collective-permute-start(f32[120,2560]{1,0:T(8,128)} %reduce-scatter.21.cloned.1.call-done), channel_id=1, source_target_pairs={{0,8},{8,0},{1,9},{9,1},{2,10},{10,2},{3,11},{11,3},{4,12},{12,4},... | collective-permute-start | bytes 3686408 | tf_op jit(solution)/shard_map/ppermute | solution.py:389
  583.4 5.7 collective-permute-start.10
  621.4 30.4 %collective-permute-start.12 = (f32[320,1024]{1,0:T(8,128)}, f32[320,1024]{1,0:T(8,128)S(1)}, u32[]{:S(2)}, u32[]{:S(2)}) collective-permute-start(f32[320,1024]{1,0:T(8,128)} %reduce-scatter.17.cloned.1.call-done), channel_id=1, source_target_pairs={{0,8},{8,0},{1,9},{9,1},{2,10},{10,2},{3,11},{11,3},{4,12},{12,4},... | collective-permute-start | bytes 3932168 | tf_op jit(solution)/shard_map/ppermute | solution.py:389
  658.6 55.2 %collective-permute-start.14 = (f32[120,5120]{1,0:T(8,128)}, f32[120,5120]{1,0:T(8,128)S(1)}, u32[]{:S(2)}, u32[]{:S(2)}) collective-permute-start(f32[120,5120]{1,0:T(8,128)} %reduce-scatter.23.cloned.1.call-done), channel_id=1, source_target_pairs={{0,8},{8,0},{1,9},{9,1},{2,10},{10,2},{3,11},{11,3},{4,12},{12,4},... | collective-permute-start | bytes 7372808 | tf_op jit(solution)/shard_map/ppermute | solution.py:389
  660.1 12.4 %copy-start.42 = (f32[320,1024]{1,0:T(8,128)S(1)}, f32[320,1024]{1,0:T(8,128)}, u32[]{:S(2)}) copy-start(f32[320,1024]{1,0:T(8,128)} %add_multiply_fusion.5) | copy-start | bytes 3932164
  677.8 36.1 %copy-start.50 = (f32[120,5120]{1,0:T(8,128)S(1)}, f32[120,5120]{1,0:T(8,128)}, u32[]{:S(2)}) copy-start(f32[120,5120]{1,0:T(8,128)} %reduce-scatter.23.cloned.1.call-done) | copy-start | bytes 7372804
  719.0 30.2 %collective-permute-start.13 = (f32[120,2688]{1,0:T(8,128)}, f32[120,2688]{1,0:T(8,128)}, u32[]{:S(2)}, u32[]{:S(2)}) collective-permute-start(f32[120,2688]{1,0:T(8,128)} %reduce-scatter.25.cloned.1.call-done), channel_id=1, source_target_pairs={{0,8},{8,0},{1,9},{9,1},{2,10},{10,2},{3,11},{11,3},{4,12},{12,4},... | collective-permute-start | bytes 3870728 | tf_op jit(solution)/shard_map/ppermute | solution.py:449
  (82 other events, 311.1 us)
Sparse Core Ops, SparseCore 0:
  10.4 76.4 all-gather.7
  89.3 36.4 all-gather.13
  128.2 35.8 all-gather.9
  165.8 56.6 all-gather.11
  224.1 37.2 all-gather.15
  287.8 57.5 reduce-scatter.14
  348.4 94.3 reduce-scatter.18
  445.8 54.8 reduce-scatter.20
  503.7 57.5 reduce-scatter.16
  564.2 94.3 reduce-scatter.22
  661.6 57.3 reduce-scatter.24

commit v3 on v2

--- a/solution.py
+++ b/solution.py
@@ -202,7 +202,7 @@
         in_specs=[pl.BlockSpec((D, seq), lambda i: (0, 0)), pl.BlockSpec((D, 256), lambda i: (0, i)), pl.BlockSpec((D, 256), lambda i: (0, steps + i))],
         out_specs=[rows, rows, rows],
         out_shape=[wide, wide, jax.ShapeDtypeStruct((FF, seq), BF16)],
-        compiler_params=pltpu.CompilerParams(dimension_semantics=('arbitrary',), vmem_limit_bytes=32 * 1024 * 1024),
+        compiler_params=pltpu.CompilerParams(dimension_semantics=('arbitrary',), vmem_limit_bytes=60 * 1024 * 1024),
         cost_estimate=pl.CostEstimate(flops=10_000_000_000, bytes_accessed=38_000_000, transcendentals=5_000_000),
         name='mlp_fwd',
     )(b, gate_up, gate_up)
@@ -230,6 +230,35 @@
         name='mlp_bwd',
     )(down, grad, gate, up)
     return out.reshape(2 * FF, seq)
+
+
+def merge_kernel(a_ref, g_ref, sent_ref, keep_ref, recv_ref, out_ref):
+    step = pl.program_id(0)
+
+    @pl.when(step < 4)
+    def _():
+        out_ref[...] = dot_nt(a_ref[...], g_ref[...]) + sent_ref[...]
+
+    @pl.when(step == 4)
+    def _():
+        out_ref[...] = keep_ref[...] + recv_ref[...]
+
+
+def merged_grad(a, g, sent, keep, recv):
+    rows, seq = a.shape
+    wide = keep.shape[1]
+    whole = pl.BlockSpec((rows, wide), lambda j: (0, 0))
+    return pl.pallas_call(
+        merge_kernel,
+        grid=(5,),
+        in_specs=[pl.BlockSpec((rows, seq), lambda j: (0, 0)), pl.BlockSpec((wide, seq), lambda j: (jnp.minimum(j, 3), 0)),
+                  pl.BlockSpec((rows, wide), lambda j: (0, jnp.minimum(j, 3))), whole, whole],
+        out_specs=pl.BlockSpec((rows, wide), lambda j: (0, j)),
+        out_shape=jax.ShapeDtypeStruct((rows, 5 * wide), F32),
+        compiler_params=pltpu.CompilerParams(dimension_semantics=('arbitrary',), vmem_limit_bytes=48 * 1024 * 1024),
+        cost_estimate=pl.CostEstimate(flops=5_000_000_000, bytes_accessed=40_000_000, transcendentals=0),
+        name='merged_grad',
+    )(a, g, sent, keep, recv)
 
 
 def gather_kernel(shard_ref, out_ref, token_ref, send_sem, recv_sem):
@@ -382,7 +411,7 @@
             l, slot, part = waiting.pop(0)
             if moving:
                 done_l, done_slot, mine, peer = moving.pop(0)
-                total = (mine + peer) * grad_scale
+                total = row_major((mine + row_major(peer)) * grad_scale)
                 value, part, outs[done_l][done_slot] = tie(value, part, total)
             else:
                 value, part = tie(value, part)
@@ -418,7 +447,10 @@
             if l == 0:
                 dmid = release(dmid)
             b_mine, dmid = tie(core_half(b, core), dmid)
-            mine_gu = row_major(dot_nt(b_mine, dgu) + sent_gu)
+            if l == 0:
+                mine_gu = merged_grad(b_mine, dgu, sent_gu, *late_attn)
+            else:
+                mine_gu = row_major(dot_nt(b_mine, dgu) + sent_gu)
             other_o = row_major(dot_nt(core_half(o, 1 - core), dmid))
             dmid, mine_gu, other_o = tie(dmid, mine_gu, other_o)
             waiting.append((l, 1, over_chips(mine_gu)))
@@ -443,27 +475,36 @@
             part = row_major(jnp.concatenate(parts, axis=1))
             grad, part = tie(grad, part)
             if l == 0:
-                part = release(release(part))
-            waiting.append((l, 0, over_chips(part)))
+                part = release(part)
+                waiting.append((l, 0, over_chips(part)))
+            else:
+                low = lax.axis_index('dp') == 0
+                left, right = part[:, :1280], part[:, 1280:]
+                other = lax.ppermute(jnp.where(low, right, left), 'dp', DP_SWAP)
+                late_attn = (jnp.where(low, left, right), other)
         (l, slot, part), = waiting
         moving.append((l, slot, part, lax.ppermute(part, 'dp', DP_SWAP)))
-        for l, slot, mine, peer in moving:
-            outs[l][slot] = (mine + peer) * grad_scale
-        ra = [o[0] for o in outs]
-        rg = [o[1] for o in outs]
+        (_, _, mine, peer), (_, _, last, last_peer) = moving
+        mine, peer = row_major(mine), row_major(peer)
+        rg0 = row_major((mine[:, :2 * FF] + peer[:, :2 * FF]) * grad_scale)
+        mine, peer = mine[:, 2 * FF:] * grad_scale, peer[:, 2 * FF:] * grad_scale
+        first = row_major(jnp.where(low, mine, peer))
+        second = row_major(jnp.where(low, peer, mine))
+        ra = row_major((row_major(last) + row_major(last_peer)) * grad_scale)
+        rg = outs[1][1]
         rd = [o[2][:, :D] for o in outs]
-        gain = ra[0][:, 2560:2564]
+        gain = ra[:, 2560:2564]
         stack = lambda parts: jnp.stack(parts)
         return (
             y.T[None], grad.T[None],
             stack([gain[:, 0], gain[:, 2]]),
-            stack([r[:, :960].reshape(rows, HEADS, HD) for r in ra]),
-            stack([r[:, 960:1280].reshape(rows, KV, HD) for r in ra]),
-            stack([r[:, 1280:1600].reshape(rows, KV, HD) for r in ra]),
-            stack([r[:, 1600:2560] for r in ra]),
+            stack([ra[:, :960].reshape(rows, HEADS, HD), first[:, :960].reshape(rows, HEADS, HD)]),
+            stack([ra[:, 960:1280].reshape(rows, KV, HD), first[:, 960:].reshape(rows, KV, HD)]),
+            stack([ra[:, 1280:1600].reshape(rows, KV, HD), second[:, :320].reshape(rows, KV, HD)]),
+            stack([ra[:, 1600:2560], second[:, 320:]]),
             stack([gain[:, 1], gain[:, 3]]),
-            stack([r[:, :FF] for r in rg]),
-            stack([r[:, FF:] for r in rg]),
+            stack([rg0[:, :FF], rg[:, :FF]]),
+            stack([rg0[:, FF:], rg[:, FF:]]),
             stack(rd),
         )
 

time: 774 us -> 787 us (1.017)
  Pallas kernels: 256 us -> 277 us
  local copies, waits for them, and re-layouts: 74.5 us -> 59.8 us
  matrix products: 187 us -> 177 us
  other arithmetic: 45.5 us -> 53.5 us
  waiting for transfers between devices: 175 us -> 183 us
    ppermute x0 -> x1, waiting for transfers between devices: none -> 33.2 us  [local_step(): other = lax.ppermute(jnp.where(low, right, left), 'dp', DP_SWAP)]
    pallas_call x0 -> x1, Pallas kernels: none -> 14.2 us  [merged_grad(): pl.pallas_call(merge_kernel, grid=(5,), in_specs=[pl.BlockSpec((rows, seq...]
    unnamed x199 -> x208, local copies, waits for them, and re-layouts: 32.1 us -> 21.6 us
    ppermute x5 -> x4, waiting for transfers between devices: 106 us -> 95.9 us  [release(): moving.append((l, slot, part, lax.ppermute(part, 'dp', DP_SWAP)))]
    dot_general x16 -> x15, matrix products: 81.7 us -> 73.5 us  [dot_nt(): lax.dot_general(a, b, (((1,), (1,)), ((), ())), preferred_element_type=F32)]
  transfers between devices with their start and end apart: 26 -> 25, of which waited for: 11 -> 9; matrix products, arithmetic and copies ran while one was open for 34% -> 32% of each run, Pallas kernels for 32% -> 34%
where the time goes in v3:
time: 787 us; the launch traced here: 776 us
  Pallas kernels  277 us (35%)
  waiting for transfers between devices  183 us (23%)
  matrix products  177 us (22%)
  local copies, waits for them, and re-layouts  59.8 us (8%)
  other arithmetic  53.5 us (7%)
  between operations  15.9 us (2%)
  starting transfers between devices  10.4 us (1%)
    ppermute x4, waiting for transfers between devices, release(): moving.append((l, slot, part, lax.ppermute(part, 'dp', DP_SWAP)))  95.9 us
    pallas_call x2, Pallas kernels, attention_backward(): pl.pallas_call(attn_bwd_kernel, grid=(KV,), in_specs=[head_spec(seq, 0, G...  89.7 us
    dot_general x15, matrix products, dot_nt(): lax.dot_general(a, b, (((1,), (1,)), ((), ())), preferred_element_type=F32)  73.5 us
    pallas_call x2, Pallas kernels, attention_forward(): pl.pallas_call(attn_fwd_kernel, grid=(KV,), in_specs=[head_spec(seq, 0, G...  58.1 us
    dot_general x6, matrix products, dot_nn(): lax.dot_general(a, b, (((1,), (0,)), ((), ())), preferred_element_type=F32)  53.9 us
    dot_general x6, matrix products, dot_tn(): lax.dot_general(a, b, (((0,), (0,)), ((), ())), preferred_element_type=F32)  49.4 us
    pallas_call x1, Pallas kernels, gather_now(): pl.pallas_call(gather_kernel, in_specs=[pl.BlockSpec(memory_space=pltpu.V...  47.6 us
    pallas_call x2, Pallas kernels, mlp_forward(): pl.pallas_call(mlp_fwd_kernel, grid=(steps,), in_specs=[pl.BlockSpec((D,...  38.3 us
  transfers between devices with their start and end apart: 25, of which 9 were waited for; matrix products, arithmetic and copies ran while one was open for 32% of the time, Pallas kernels for 34%

profile of v3, /device:TPU:0, one launch (start us, length us, event | category | flops | bytes accessed | tf_op | source)
XLA Modules:
  0.0 776.5 jit_solution(11408639087521372851)
XLA Ops:
  19.0 47.6 %gather_attn0.1 = (bf16[8,120,2688]{2,1,0:T(8,128)(2,1)S(1)}, f32[8,128]{1,0:T(8,128)}) custom-call(bf16[120,2688]{1,0:T(8,128)(2,1)S(1)} %concatenate.24.shard_ref), custom_call_target="tpu_custom_call" | custom-call | tf_op jit(solution)/shard_map/gather_attn0/pallas_call | solution.py:311
  71.5 5.6 fusion.52.q_ref.k_ref.v_ref
  77.7 28.9 %attn_fwd.2 = (bf16[960,1024]{1,0:T(8,128)(2,1)S(1)}, bf16[320,1024]{1,0:T(8,128)(2,1)S(1)}, bf16[320,1024]{1,0:T(8,128)(2,1)S(1)}, bf16[960,1024]{1,0:T(8,128)(2,1)S(1)}) custom-call(f32[1600,1024]{1,0:T(8,128)} %fusion.52.q_ref.k_ref.v_ref, f32[1600,1024]{1,0:T(8,128)} %fusion.52.q_ref.k_ref.v_ref, f32[1600,1024]{1,0:T(8,128)} %fusion.52.q_ref.k_ref.v_ref, ...), custom_call_target="tpu_custom_call" | custom-call | flops 20000000000 | bytes 14000000 | tf_op jit(solution)/shard_map/attn_fwd/pallas_call | solution.py:156
  106.7 5.4 fusion.39
  112.7 3.3 fusion.14.b_ref
  116.0 19.0 %mlp_fwd.2 = (f32[2560,1024]{1,0:T(8,128)}, f32[2560,1024]{1,0:T(8,128)}, bf16[2560,1024]{1,0:T(8,128)(2,1)}) custom-call(bf16[960,1024]{1,0:T(8,128)(2,1)} %fusion.14.b_ref, bf16[960,5120]{1,0:T(8,128)(2,1)} %all-gather.8.cloned.1.call-done.wg_ref.wu_ref, bf16[960,5120]{1,0:T(8,128)(2,1)} %all-gather.8.cloned.1.call-done.wg_ref.wu_ref), custom_call_target="tpu_custom_call" | custom-call | flops 10000000000 | bytes 38000000 | tf_op jit(solution)/shard_map/mlp_fwd/pallas_call | solution.py:199
  135.0 10.5 %fusion.42 = (f32[1024]{0:T(1024)S(1)}, bf16[960,1024]{1,0:T(8,128)(2,1)S(1)}, f32[1024,960]{0,1:T(8,128)}) fusion(bf16[960,1024]{1,0:T(8,128)(2,1)S(1)} %copy-done.28, bf16[2560,1024]{1,0:T(8,128)(2,1)} %get-tuple-element.93, bf16[1,2560,960]{2,1,0:T(8,128)(2,1)} %all-gather.14.cloned.1.call-done), kind=kOutput, calls=%fused_computation.70 | convolution fusion | flops 5039062016 | bytes 18026496 | tf_op jit(solution)/shard_map/dot_general | solution.py:52
  147.2 16.9 %all-gather.10.cloned.1.call-done = bf16[960,2560]{1,0:T(8,128)(2,1)} async-done(((bf16[120,2560]{1,0:T(8,128)(2,1)}), bf16[960,2560]{1,0:T(8,128)(2,1)}) %all-gather.10.cloned.1.call-update) | async-done | bytes 4915216 | tf_op jit(solution)/shard_map/all_gather | solution.py:358
  164.1 7.5 fusion.48.q_ref.k_ref.v_ref
  171.6 29.2 %attn_fwd.3 = (bf16[960,1024]{1,0:T(8,128)(2,1)S(1)}, bf16[320,1024]{1,0:T(8,128)(2,1)S(1)}, bf16[320,1024]{1,0:T(8,128)(2,1)S(1)}, bf16[960,1024]{1,0:T(8,128)(2,1)S(1)}) custom-call(f32[1600,1024]{1,0:T(8,128)} %fusion.48.q_ref.k_ref.v_ref, f32[1600,1024]{1,0:T(8,128)} %fusion.48.q_ref.k_ref.v_ref, f32[1600,1024]{1,0:T(8,128)} %fusion.48.q_ref.k_ref.v_ref, ...), custom_call_target="tpu_custom_call" | custom-call | flops 20000000000 | bytes 14000000 | tf_op jit(solution)/shard_map/attn_fwd/pallas_call | solution.py:156
  200.8 7.8 fusion.37
  211.6 10.9 %all-gather.12.cloned.1.call-done.wg_ref.wu_ref = bf16[960,5120]{1,0:T(8,128)(2,1)} async-done(((bf16[120,5120]{1,0:T(8,128)(2,1)}), bf16[960,5120]{1,0:T(8,128)(2,1)}) %all-gather.12.cloned.1.call-update) | async-done | bytes 9830416 | tf_op jit(solution)/shard_map/all_gather | solution.py:358
  222.5 19.3 %mlp_fwd.3 = (f32[2560,1024]{1,0:T(8,128)}, f32[2560,1024]{1,0:T(8,128)}, bf16[2560,1024]{1,0:T(8,128)(2,1)}) custom-call(bf16[960,1024]{1,0:T(8,128)(2,1)} %fusion.15.b_ref, bf16[960,5120]{1,0:T(8,128)(2,1)} %all-gather.12.cloned.1.call-done.wg_ref.wu_ref, bf16[960,5120]{1,0:T(8,128)(2,1)} %all-gather.12.cloned.1.call-done.wg_ref.wu_ref), custom_call_target="tpu_custom_call" | custom-call | flops 10000000000 | bytes 38000000 | tf_op jit(solution)/shard_map/mlp_fwd/pallas_call | solution.py:199
  241.8 4.1 constant_dynamic-slice_fusion.12
  250.4 8.2 %collective-permute-done = f32[1280,1024]{1,0:T(8,128)S(1)} collective-permute-done((f32[1280,1024]{1,0:T(8,128)S(1)}, f32[1280,1024]{1,0:T(8,128)S(1)}, u32[]{:S(2)}, u32[]{:S(2)}) %collective-permute-start) | collective-permute-done | bytes 5242912 | tf_op jit(solution)/shard_map/ppermute | solution.py:342
  258.6 4.8 convolution_add_fusion.2
  265.9 14.3 %mlp_bwd.2 = bf16[2,2560,1024]{2,1,0:T(8,128)(2,1)S(1)} custom-call(bf16[2560,960]{1,0:T(8,128)(2,1)S(1)} %bitcast.216, bf16[960,1024]{1,0:T(8,128)(2,1)S(1)} %bitcast.214, f32[2560,1024]{1,0:T(8,128)} %get-tuple-element.106.gate_ref, f32[2560,1024]{1,0:T(8,128)} %get-tuple-element.107.up_ref), custom_call_target="tpu_custom_call" | custom-call | flops 5000000000 | bytes 38000000 | tf_op jit(solution)/shard_map/mlp_bwd/pallas_call | solution.py:222
  280.2 7.7 fusion.98
  291.2 18.3 %fusion.29 = (f32[960]{0:T(1024)}, f32[1024]{0:T(1024)S(1)}, bf16[960,1024]{1,0:T(8,128)(2,1)S(1)}) fusion(bf16[960,1024]{1,0:T(8,128)(2,1)S(1)} %copy-done.34, f32[1024]{0:T(1024)S(1)} %add_rsqrt_fusion, f32[960]{0:T(1024)S(1)} %bitcast.278, bf16[960,5120]{1,0:T(8,128)(2,1)} %all-gather.12.cloned.1.call-done.wg_ref.wu_ref, bf16[5120,1024]{1,0:T(8,128)(2,1)} %bitcast.208), kind=kOutput, calls=%fused_computation.57 | convolution fusion | flops 10075174912 | bytes 24264192 | tf_op jit(solution)/shard_map/dot_general | solution.py:44
  313.2 10.2 %convolution_add_fusion = f32[480,5120]{1,0:T(8,128)} fusion(f32[480,5120]{1,0:T(8,128)} %collective-permute-done.1, bf16[480,1024]{1,0:T(8,128)(2,1)S(1)} %bitcast.252, bf16[5120,1024]{1,0:T(8,128)(2,1)S(1)} %bitcast.211), kind=kOutput, calls=%fused_computation.10 | convolution fusion | flops 5035622400 | bytes 31129600 | tf_op jit(solution)/shard_map/dot_general | solution.py:48
  326.7 5.1 convolution_convert_fusion.3.do_ref
  331.8 44.7 %attn_bwd.2 = (bf16[960,1024]{1,0:T(8,128)(2,1)S(1)}, bf16[320,1024]{1,0:T(8,128)(2,1)S(1)}, bf16[320,1024]{1,0:T(8,128)(2,1)S(1)}) custom-call(bf16[960,1024]{1,0:T(8,128)(2,1)} %copy-done.12, bf16[320,1024]{1,0:T(8,128)(2,1)S(1)} %get-tuple-element.114.k_ref, bf16[320,1024]{1,0:T(8,128)(2,1)S(1)} %copy-done.18, ...), custom_call_target="tpu_custom_call" | custom-call | flops 40000000000 | bytes 14000000 | tf_op jit(solution)/shard_map/attn_bwd/pallas_call | solution.py:173
  382.1 3.8 fusion.101
  390.2 4.9 fusion.30
  396.3 4.7 convolution_add_fusion.4
  404.1 4.8 fusion.57
  409.5 14.9 %mlp_bwd.3 = bf16[2,2560,1024]{2,1,0:T(8,128)(2,1)S(1)} custom-call(bf16[2560,960]{1,0:T(8,128)(2,1)S(1)} %bitcast.219, bf16[960,1024]{1,0:T(8,128)(2,1)S(1)} %fusion.25.grad_ref, f32[2560,1024]{1,0:T(8,128)} %get-tuple-element.131.gate_ref, f32[2560,1024]{1,0:T(8,128)} %get-tuple-element.132.up_ref), custom_call_target="tpu_custom_call" | custom-call | flops 5000000000 | bytes 38000000 | tf_op jit(solution)/shard_map/mlp_bwd/pallas_call | solution.py:222
  424.4 7.7 fusion.102
  432.1 4.8 convolution_add_fusion.1
  439.0 3.1 constant_dynamic-slice_fusion.4
  442.2 26.4 %collective-permute-done.5 = f32[320,1024]{1,0:T(8,128)} collective-permute-done((f32[320,1024]{1,0:T(8,128)}, f32[320,1024]{1,0:T(8,128)}, u32[]{:S(2)}, u32[]{:S(2)}) %collective-permute-start.5) | collective-permute-done | bytes 1310752 | tf_op jit(solution)/shard_map/ppermute | solution.py:418
  471.4 5.3 slice_select_fusion
  478.2 14.5 %fusion.31 = (f32[960]{0:T(1024)S(1)}, f32[1024]{0:T(1024)S(1)}, bf16[960,1024]{1,0:T(8,128)(2,1)S(1)}) fusion(bf16[960,1024]{1,0:T(8,128)(2,1)S(1)} %copy-done.29, f32[1024]{0:T(1024)S(1)} %copy-done.72, f32[960]{0:T(1024)S(1)} %bitcast.272, bf16[960,5120]{1,0:T(8,128)(2,1)} %all-gather.8.cloned.1.call-done.wg_ref.wu_ref, bf16[5120,1024]{1,0:T(8,128)(2,1)S(1)} %bitcast.206), kind=kOutput, calls=%fused_computation.59 | convolution fusion | flops 10075174912 | bytes 24264192 | tf_op jit(solution)/shard_map/dot_general | solution.py:44
  494.0 4.4 fusion.103
  498.4 33.2 %collective-permute-done.7.recv_ref = f32[480,1280]{1,0:T(8,128)} collective-permute-done((f32[480,1280]{1,0:T(8,128)}, f32[480,1280]{1,0:T(8,128)}, u32[]{:S(2)}, u32[]{:S(2)}) %collective-permute-start.7) | collective-permute-done | bytes 2457632 | tf_op jit(solution)/shard_map/ppermute | solution.py:483
  531.6 14.2 %merged_grad.1 = f32[480,6400]{1,0:T(8,128)} custom-call(bf16[480,1024]{1,0:T(8,128)(2,1)S(1)} %bitcast.220, bf16[5120,1024]{1,0:T(8,128)(2,1)} %bitcast.203, f32[480,5120]{1,0:T(8,128)} %collective-permute-done.6.sent_ref, f32[480,1280]{1,0:T(8,128)S(1)} %copy-done.4, f32[480,1280]{1,0:T(8,128)} %collective-permute-done.7.recv_ref), custom_call_target="tpu_custom_call" | custom-call | flops 5000000000 | bytes 40000000 | tf_op jit(solution)/shard_map/merged_grad/pallas_call | solution.py:251
  550.3 5.7 convolution_convert_fusion.2.do_ref
  556.0 45.0 %attn_bwd.3 = (bf16[960,1024]{1,0:T(8,128)(2,1)S(1)}, bf16[320,1024]{1,0:T(8,128)(2,1)S(1)}, bf16[320,1024]{1,0:T(8,128)(2,1)S(1)}) custom-call(bf16[960,1024]{1,0:T(8,128)(2,1)} %copy-done.11, bf16[320,1024]{1,0:T(8,128)(2,1)S(1)} %copy-done.14, bf16[320,1024]{1,0:T(8,128)(2,1)S(1)} %copy-done.16, bf16[960,1024]{1,0:T(8,128)(2,1)} %convolution_convert_fusion.2.do_ref, ...), custom_call_target="tpu_custom_call" | custom-call | flops 40000000000 | bytes 14000000 | tf_op jit(solution)/shard_map/attn_bwd/pallas_call | solution.py:173
  605.6 4.5 convolution_add_fusion.5
  610.1 3.7 fusion.104
  614.8 5.5 fusion.32
  622.1 4.0 fusion.19
  626.1 19.3 %collective-permute-done.12 = f32[320,1024]{1,0:T(8,128)} collective-permute-done((f32[320,1024]{1,0:T(8,128)}, f32[320,1024]{1,0:T(8,128)}, u32[]{:S(2)}, u32[]{:S(2)}) %collective-permute-start.12) | collective-permute-done | bytes 1310752 | tf_op jit(solution)/shard_map/ppermute | solution.py:418
  648.5 5.7 convolution_add_fusion.3
  654.2 6.5 concatenate.31
  662.5 12.7 %fusion.55 = bf16[1,1024,960]{1,2,0:T(8,128)(2,1)} fusion(f32[960,1024]{1,0:T(8,128)} %get-tuple-element.231, f32[1024,960]{0,1:T(8,128)} %get-tuple-element.230, f32[960,1024]{1,0:T(8,128)} %get-tuple-element.229, bf16[1,1024,960]{1,2,0:T(8,128)(2,1)S(1)} %copy-done.20, bf16[2560,1024]{1,0:T(8,128)(2,1)} %get-tuple-element.101, ...), kind=kOutput, calls=%fused_computation.97 | convolution fusion | flops 5044961280 | bytes 25886720 | tf_op jit(solution)/shard_map/dot_general | solution.py:52
  679.1 50.2 %collective-permute-done.14 = f32[120,6400]{1,0:T(8,128)S(1)} collective-permute-done((f32[120,6400]{1,0:T(8,128)}, f32[120,6400]{1,0:T(8,128)S(1)}, u32[]{:S(2)}, u32[]{:S(2)}) %collective-permute-start.14) | collective-permute-done | bytes 3072032 | tf_op jit(solution)/shard_map/ppermute | solution.py:418
  744.8 17.2 %collective-permute-done.13 = f32[120,2688]{1,0:T(8,128)} collective-permute-done((f32[120,2688]{1,0:T(8,128)}, f32[120,2688]{1,0:T(8,128)}, u32[]{:S(2)}, u32[]{:S(2)}) %collective-permute-start.13) | collective-permute-done | bytes 1290272 | tf_op jit(solution)/shard_map/ppermute | solution.py:486
  (365 shorter events, 104.7 us)
Async XLA Ops:
  7.2 108.8 %all-gather.8.cloned.1.call-start = ((), (), s32[]{:S(2)}) async-start(), calls=%async_computation.5 | async-start | bytes 11059200 | tf_op jit(solution)/shard_map/all_gather | solution.py:358
  9.9 125.1 %all-gather.14.cloned.1.call-start = ((), (), s32[]{:S(2)}) async-start(), calls=%async_computation.10 | async-start | bytes 5898240 | tf_op jit(solution)/shard_map/all_gather | solution.py:358
  10.8 153.3 %all-gather.10.cloned.1.call-start = ((), (), s32[]{:S(2)}) async-start(), calls=%async_computation.6 | async-start | bytes 5529600 | tf_op jit(solution)/shard_map/all_gather | solution.py:358
  13.6 208.9 %all-gather.12.cloned.1.call-start = ((), (), s32[]{:S(2)}) async-start(), calls=%async_computation.7 | async-start | bytes 11059200 | tf_op jit(solution)/shard_map/all_gather | solution.py:358
  15.1 54.0 %copy-start.19 = (bf16[1,1024,960]{1,2,0:T(8,128)(2,1)S(1)}, bf16[1,1024,960]{1,2,0:T(8,128)(2,1)}, u32[]{:S(2)}) copy-start(bf16[1,1024,960]{1,2,0:T(8,128)(2,1)} %param.11) | copy-start | bytes 5898244
  15.1 248.3 %all-gather.16.cloned.1.call-start = ((), (), s32[]{:S(2)}) async-start(), calls=%async_computation.11 | async-start | bytes 5898240 | tf_op jit(solution)/shard_map/all_gather | solution.py:358
  17.3 361.7 %reduce-scatter.12.cloned.1.call-start = ((), (), s32[]{:S(2)}) async-start(), calls=%async_computation.8 | async-start | bytes 6553600 | tf_op jit(solution)/shard_map/reduce_scatter | solution.py:350
  69.1 43.0 %copy-start.77 = (f32[960,1]{0,1:T(1,128)}, f32[960,1]{0,1:T(1,128)S(1)}, u32[]{:S(2)}) copy-start(f32[960,1]{0,1:T(1,128)S(1)} %get-tuple-element.221) | copy-start | bytes 11524
  69.1 76.4 %copy-start.79 = (f32[960,1]{0,1:T(1,128)}, f32[960,1]{0,1:T(1,128)S(1)}, u32[]{:S(2)}) copy-start(f32[960,1]{0,1:T(1,128)S(1)} %get-tuple-element.220) | copy-start | bytes 11524
  112.1 22.9 %copy-start.81 = (f32[1024]{0:T(1024)}, f32[1024]{0:T(1024)S(1)}, u32[]{:S(2)}) copy-start(f32[1024]{0:T(1024)S(1)} %get-tuple-element.187) | copy-start | bytes 12292
  116.0 19.0 %copy-start.28 = (bf16[960,1024]{1,0:T(8,128)(2,1)S(1)}, bf16[960,1024]{1,0:T(8,128)(2,1)}, u32[]{:S(2)}) copy-start(bf16[960,1024]{1,0:T(8,128)(2,1)} %get-tuple-element.188) | copy-start | bytes 5898244
  145.5 18.7 %copy-start.83 = (f32[1024]{0:T(1024)}, f32[1024]{0:T(1024)S(1)}, u32[]{:S(2)}) copy-start(f32[1024]{0:T(1024)S(1)} %get-tuple-element.185) | copy-start | bytes 12292
  145.5 18.7 %copy-start.73 = (f32[1024]{0:T(1024)}, f32[1024]{0:T(1024)S(1)}, u32[]{:S(2)}) copy-start(f32[1024]{0:T(1024)S(1)} %add_rsqrt_fusion.1) | copy-start | bytes 12292
  147.2 24.4 %copy-start.25 = (bf16[960,1024]{1,0:T(8,128)(2,1)}, bf16[960,1024]{1,0:T(8,128)(2,1)S(1)}, u32[]{:S(2)}) copy-start(bf16[960,1024]{1,0:T(8,128)(2,1)S(1)} %fusion.13) | copy-start | bytes 5898244
  171.6 29.2 %copy-start.31 = (bf16[960,1024]{1,0:T(8,128)(2,1)S(1)}, bf16[960,1024]{1,0:T(8,128)(2,1)}, u32[]{:S(2)}) copy-start(bf16[960,1024]{1,0:T(8,128)(2,1)} %copy-done.30) | copy-start | bytes 5898244
  248.9 9.7 %collective-permute-start = (f32[1280,1024]{1,0:T(8,128)S(1)}, f32[1280,1024]{1,0:T(8,128)S(1)}, u32[]{:S(2)}, u32[]{:S(2)}) collective-permute-start(f32[1280,1024]{1,0:T(8,128)S(1)} %fusion.60), channel_id=1, source_target_pairs={{0,1},{1,0},{2,3},{3,2},{4,5},{5,4},{6,7},{7,6},{8,9},{9,8},{10,11... | collective-permute-start | bytes 15728648 | tf_op jit(solution)/shard_map/ppermute | solution.py:342
  288.0 25.2 %collective-permute-start.1 = (f32[480,5120]{1,0:T(8,128)}, f32[480,5120]{1,0:T(8,128)}, u32[]{:S(2)}, u32[]{:S(2)}) collective-permute-start(f32[480,5120]{1,0:T(8,128)} %fusion.98), channel_id=1, source_target_pairs={{0,1},{1,0},{2,3},{3,2},{4,5},{5,4},{6,7},{7,6},{8,9},{9,8},{10,11... | collective-permute-start | bytes 29491208 | tf_op jit(solution)/shard_map/ppermute | solution.py:342
  288.3 205.6 %reduce-scatter.16.cloned.1.call-start = ((), (), s32[]{:S(2)}) async-start(), calls=%async_computation.12 | async-start | bytes 12288000
  288.4 24.8 %slice-start.3 = ((s8[10485760]{0:T(1024)(128)(4,1)}), s8[4194304]{0:T(1024)(128)(4,1)S(1)}, s32[]{:S(2)}) async-start(s8[10485760]{0:T(1024)(128)(4,1)} %bitcast.209), calls=%async_computation.18 | async-start | bytes 8388608
  291.2 21.9 %slice-start.4 = ((s8[10485760]{0:T(1024)(128)(4,1)}), s8[4194304]{0:T(1024)(128)(4,1)S(1)}, s32[]{:S(2)}) async-start(s8[10485760]{0:T(1024)(128)(4,1)} %bitcast.209), calls=%async_computation.19 | async-start | bytes 8388608
  291.2 22.0 %slice-start.5 = ((s8[10485760]{0:T(1024)(128)(4,1)}), s8[2097152]{0:T(1024)(128)(4,1)S(1)}, s32[]{:S(2)}) async-start(s8[10485760]{0:T(1024)(128)(4,1)} %bitcast.209), calls=%async_computation.20 | async-start | bytes 4194304
  323.4 282.1 %reduce-scatter.14.cloned.1.call-start = ((), (), s32[]{:S(2)}) async-start(), calls=%async_computation.9 | async-start | bytes 6553600 | tf_op jit(solution)/shard_map/reduce_scatter | solution.py:350
  326.5 59.5 %collective-permute-start.2 = (f32[480,960]{1,0:T(8,128)}, f32[480,960]{1,0:T(8,128)}, u32[]{:S(2)}, u32[]{:S(2)}) collective-permute-start(f32[480,960]{1,0:T(8,128)} %fusion.99), channel_id=1, source_target_pairs={{0,1},{1,0},{2,3},{3,2},{4,5},{5,4},{6,7},{7,6},{8,9},{9,8},{10,11... | collective-permute-start | bytes 5529608 | tf_op jit(solution)/shard_map/ppermute | solution.py:342
  388.2 8.1 %collective-permute-start.3 = (f32[480,1600]{1,0:T(8,128)}, f32[480,1600]{1,0:T(8,128)}, u32[]{:S(2)}, u32[]{:S(2)}) collective-permute-start(f32[480,1600]{1,0:T(8,128)} %fusion.101), channel_id=1, source_target_pairs={{0,1},{1,0},{2,3},{3,2},{4,5},{5,4},{6,7},{7,6},{8,9},{9,8},{10,11... | collective-permute-start | bytes 9216008 | tf_op jit(solution)/shard_map/ppermute | solution.py:342
  396.3 35.9 %copy-start.1 = (bf16[960,1024]{1,0:T(8,128)(2,1)}, bf16[960,1024]{1,0:T(8,128)(2,1)S(1)}, u32[]{:S(2)}) copy-start(bf16[960,1024]{1,0:T(8,128)(2,1)S(1)} %fusion.25.grad_ref) | copy-start | bytes 5898244
  408.9 23.3 %collective-permute-start.4 = (f32[1280,1024]{1,0:T(8,128)}, f32[1280,1024]{1,0:T(8,128)S(1)}, u32[]{:S(2)}, u32[]{:S(2)}) collective-permute-start(f32[1280,1024]{1,0:T(8,128)} %fusion.57), channel_id=1, source_target_pairs={{0,1},{1,0},{2,3},{3,2},{4,5},{5,4},{6,7},{7,6},{8,9},{9,8},{10,11... | collective-permute-start | bytes 15728648 | tf_op jit(solution)/shard_map/ppermute | solution.py:342
  436.9 41.3 %slice-start = ((s8[10485760]{0:T(1024)(128)(4,1)}), s8[2097152]{0:T(1024)(128)(4,1)S(1)}, s32[]{:S(2)}) async-start(s8[10485760]{0:T(1024)(128)(4,1)} %bitcast.204), calls=%async_computation.15 | async-start | bytes 4194304
  437.0 224.0 %reduce-scatter.18.cloned.1.call-start = ((), (), s32[]{:S(2)}) async-start(), calls=%async_computation.13 | async-start | bytes 15360000
  437.0 94.6 %collective-permute-start.6 = (f32[480,5120]{1,0:T(8,128)}, f32[480,5120]{1,0:T(8,128)}, u32[]{:S(2)}, u32[]{:S(2)}) collective-permute-start(f32[480,5120]{1,0:T(8,128)} %fusion.102), channel_id=1, source_target_pairs={{0,1},{1,0},{2,3},{3,2},{4,5},{5,4},{6,7},{7,6},{8,9},{9,8},{10,11... | collective-permute-start | bytes 29491208 | tf_op jit(solution)/shard_map/ppermute | solution.py:342
  437.4 31.2 %collective-permute-start.5 = (f32[320,1024]{1,0:T(8,128)}, f32[320,1024]{1,0:T(8,128)}, u32[]{:S(2)}, u32[]{:S(2)}) collective-permute-start(f32[320,1024]{1,0:T(8,128)} %reduce-scatter.12.cloned.1.call-done), channel_id=1, source_target_pairs={{0,8},{8,0},{1,9},{9,1},{2,10},{10,2},{3,11},{11,3},{4,12},{12,4},... | collective-permute-start | bytes 3932168 | tf_op jit(solution)/shard_map/ppermute | solution.py:418
  439.0 29.5 %copy-start.54 = (f32[320,1024]{1,0:T(8,128)S(1)}, f32[320,1024]{1,0:T(8,128)}, u32[]{:S(2)}) copy-start(f32[320,1024]{1,0:T(8,128)} %reduce-scatter.12.cloned.1.call-done) | copy-start | bytes 3932164
  439.0 39.2 %slice-start.1 = ((s8[10485760]{0:T(1024)(128)(4,1)}), s8[4194304]{0:T(1024)(128)(4,1)S(1)}, s32[]{:S(2)}) async-start(s8[10485760]{0:T(1024)(128)(4,1)} %bitcast.204), calls=%async_computation.16 | async-start | bytes 8388608
  476.7 16.1 %copy-start.82 = (f32[1024]{0:T(1024)S(1)}, f32[1024]{0:T(1024)}, u32[]{:S(2)}) copy-start(f32[1024]{0:T(1024)} %copy-done.81) | copy-start | bytes 12292
  476.7 16.1 %copy-start.2 = (bf16[960,1024]{1,0:T(8,128)(2,1)S(1)}, bf16[960,1024]{1,0:T(8,128)(2,1)}, u32[]{:S(2)}) copy-start(bf16[960,1024]{1,0:T(8,128)(2,1)} %copy-done.1) | copy-start | bytes 5898244
  476.7 54.9 %collective-permute-start.7 = (f32[480,1280]{1,0:T(8,128)}, f32[480,1280]{1,0:T(8,128)}, u32[]{:S(2)}, u32[]{:S(2)}) collective-permute-start(f32[480,1280]{1,0:T(8,128)} %get-tuple-element.195), channel_id=1, source_target_pairs={{0,8},{8,0},{1,9},{9,1},{2,10},{10,2},{3,11},{11,3},{4,12},{12,4},... | collective-permute-start | bytes 7372808 | tf_op jit(solution)/shard_map/ppermute | solution.py:483
  493.9 37.7 %copy-start.4 = (f32[480,1280]{1,0:T(8,128)S(1)}, f32[480,1280]{1,0:T(8,128)}, u32[]{:S(2)}) copy-start(f32[480,1280]{1,0:T(8,128)} %get-tuple-element.196.keep_ref) | copy-start | bytes 7372804
  545.9 186.8 %reduce-scatter.20.cloned.1.call-start = ((), (), s32[]{:S(2)}) async-start(), calls=%async_computation.14 | async-start | bytes 6451200
  548.9 54.0 %collective-permute-start.8 = (f32[120,5120]{1,0:T(8,128)}, f32[120,5120]{1,0:T(8,128)S(1)}, u32[]{:S(2)}, u32[]{:S(2)}) collective-permute-start(f32[120,5120]{1,0:T(8,128)} %reduce-scatter.16.cloned.1.call-done), channel_id=1, source_target_pairs={{0,8},{8,0},{1,9},{9,1},{2,10},{10,2},{3,11},{11,3},{4,12},{12,4},... | collective-permute-start | bytes 7372808 | tf_op jit(solution)/shard_map/ppermute | solution.py:418
  550.3 55.3 %collective-permute-start.9 = (f32[480,960]{1,0:T(8,128)}, f32[480,960]{1,0:T(8,128)}, u32[]{:S(2)}, u32[]{:S(2)}) collective-permute-start(f32[480,960]{1,0:T(8,128)} %fusion.103), channel_id=1, source_target_pairs={{0,1},{1,0},{2,3},{3,2},{4,5},{5,4},{6,7},{7,6},{8,9},{9,8},{10,11... | collective-permute-start | bytes 5529608 | tf_op jit(solution)/shard_map/ppermute | solution.py:342
  613.8 34.7 %collective-permute-start.10 = (f32[480,1600]{1,0:T(8,128)}, f32[480,1600]{1,0:T(8,128)}, u32[]{:S(2)}, u32[]{:S(2)}) collective-permute-start(f32[480,1600]{1,0:T(8,128)} %fusion.104), channel_id=1, source_target_pairs={{0,1},{1,0},{2,3},{3,2},{4,5},{5,4},{6,7},{7,6},{8,9},{9,8},{10,11... | collective-permute-start | bytes 9216008 | tf_op jit(solution)/shard_map/ppermute | solution.py:342
  614.4 31.0 %collective-permute-start.12 = (f32[320,1024]{1,0:T(8,128)}, f32[320,1024]{1,0:T(8,128)}, u32[]{:S(2)}, u32[]{:S(2)}) collective-permute-start(f32[320,1024]{1,0:T(8,128)} %reduce-scatter.14.cloned.1.call-done), channel_id=1, source_target_pairs={{0,8},{8,0},{1,9},{9,1},{2,10},{10,2},{3,11},{11,3},{4,12},{12,4},... | collective-permute-start | bytes 3932168 | tf_op jit(solution)/shard_map/ppermute | solution.py:418
  620.6 5.5 collective-permute-start.11
  626.1 22.4 %copy-start.46 = (bf16[1600,1024]{1,0:T(8,128)(2,1)S(1)}, bf16[1600,1024]{1,0:T(8,128)(2,1)}, u32[]{:S(2)}) copy-start(bf16[1600,1024]{1,0:T(8,128)(2,1)} %pad_maximum_fusion.2) | copy-start | bytes 9830404
  626.1 22.4 %copy-start.59 = (bf16[4,1,120,1024]{3,2,1,0:T(8,128)(2,1)S(1)}, bf16[4,1,120,1024]{3,2,1,0:T(8,128)(2,1)}, u32[]{:S(2)}) copy-start(bf16[4,1,120,1024]{3,2,1,0:T(8,128)(2,1)} %get-tuple-element.202) | copy-start | bytes 2949124
  661.0 68.3 %collective-permute-start.14 = (f32[120,6400]{1,0:T(8,128)}, f32[120,6400]{1,0:T(8,128)S(1)}, u32[]{:S(2)}, u32[]{:S(2)}) collective-permute-start(f32[120,6400]{1,0:T(8,128)} %reduce-scatter.18.cloned.1.call-done), channel_id=1, source_target_pairs={{0,8},{8,0},{1,9},{9,1},{2,10},{10,2},{3,11},{11,3},{4,12},{12,4},... | collective-permute-start | bytes 9216008 | tf_op jit(solution)/shard_map/ppermute | solution.py:418
  677.4 51.9 %copy-start.48 = (f32[120,6400]{1,0:T(8,128)S(1)}, f32[120,6400]{1,0:T(8,128)}, u32[]{:S(2)}) copy-start(f32[120,6400]{1,0:T(8,128)} %reduce-scatter.18.cloned.1.call-done) | copy-start | bytes 9216004
  732.7 29.4 %collective-permute-start.13 = (f32[120,2688]{1,0:T(8,128)}, f32[120,2688]{1,0:T(8,128)}, u32[]{:S(2)}, u32[]{:S(2)}) collective-permute-start(f32[120,2688]{1,0:T(8,128)} %reduce-scatter.20.cloned.1.call-done), channel_id=1, source_target_pairs={{0,8},{8,0},{1,9},{9,1},{2,10},{10,2},{3,11},{11,3},{4,12},{12,4},... | collective-permute-start | bytes 3870728 | tf_op jit(solution)/shard_map/ppermute | solution.py:486
  743.2 18.8 %copy-start.55 = (f32[120,2688]{1,0:T(8,128)S(1)}, f32[120,2688]{1,0:T(8,128)}, u32[]{:S(2)}) copy-start(f32[120,2688]{1,0:T(8,128)} %reduce-scatter.20.cloned.1.call-done) | copy-start | bytes 3870724
  (86 other events, 375.9 us)
Sparse Core Ops, SparseCore 0:
  10.4 76.4 all-gather.7
  89.3 36.4 all-gather.13
  128.2 35.8 all-gather.9
  165.8 56.6 all-gather.11
  224.2 37.2 all-gather.15
  288.5 57.5 reduce-scatter.11
  349.2 94.3 reduce-scatter.15
  446.5 57.5 reduce-scatter.13
  546.0 114.9 reduce-scatter.17
  663.8 57.3 reduce-scatter.19
